TPU v7x, 256 devices: a whole 4x4x8 slice. The times are simulated.
256 devices in a mesh: data: 256 (over z, y, x, core).
Axes of the slice: x: 4, y: 4, z: 8, core: 2. Of those that a mesh axis runs over, the one named last changes fastest.
Arguments:
- z_one: bfloat16 [16384, 256], P('data')
- z_two: bfloat16 [16384, 256], P('data')
- protos: bfloat16 [8192, 256], replicated
- queue_one: bfloat16 [131072, 256], P('data')
- queue_two: bfloat16 [131072, 256], P('data')
Outputs:
- output 1: float32 [16384, 8192], P('data')
- output 2: float32 [16384, 8192], P('data')
- output 3: float32 [], replicated
- output 4: float32 [16384, 256], P('data')
- output 5: float32 [16384, 256], P('data')
- output 6: float32 [8192, 256], replicated
All inputs are finite; a program needn't handle non-finite values.
Results may differ from a plain program's by a relative error of at most 0.001.
Values are sent between devices in bfloat16 or wider.
A program may use at most 768 MiB of HBM per device.

v0:
```python
import jax
import jax.numpy as jnp
from jax import lax
from jax.sharding import PartitionSpec as P

EPSILON = 0.05
value_a11 = 0.1
value_a14 = 3


def view_codes(own_rows, protos, batch_rows, total_rows):
    protos_count = protos.shape[0]
    scores = jnp.einsum("nd,kd->nk", own_rows, protos, preferred_element_type=jnp.float32)
    transport = jnp.exp(scores / EPSILON)
    for _ in range(value_a14 - 1):
        col_sum = lax.psum(jnp.sum(transport, axis=0), "data")
        transport = transport / (protos_count * col_sum)
        transport = transport / (total_rows * jnp.sum(transport, axis=1, keepdims=True))
    col_sum = lax.psum(jnp.sum(transport, axis=0), "data")
    plan_batch = transport[:batch_rows] / (protos_count * col_sum)
    return plan_batch / jnp.sum(plan_batch, axis=1, keepdims=True), scores[:batch_rows]


def solution(mesh):
    group_size = mesh.shape["data"]

    def local_step(z_one, z_two, protos, queue_one, queue_two):
        batch_rows = z_one.shape[0]
        total_rows = group_size * (batch_rows + queue_one.shape[0])
        batch_total = group_size * batch_rows
        codes_one, score_one = view_codes(jnp.concatenate([z_one, queue_one], axis=0), protos, batch_rows, total_rows)
        codes_two, score_two = view_codes(jnp.concatenate([z_two, queue_two], axis=0), protos, batch_rows, total_rows)
        logp_one = jax.nn.log_softmax(score_one / value_a11, axis=1)
        logp_two = jax.nn.log_softmax(score_two / value_a11, axis=1)
        part_loss = jnp.sum(codes_two * logp_one) + jnp.sum(codes_one * logp_two)
        swap_loss = -lax.psum(part_loss, "data") / (2 * batch_total)
        grad_coef = 1.0 / (2 * batch_total * value_a11)
        grad_s_one = ((jnp.exp(logp_one) - codes_two) * grad_coef).astype(jnp.bfloat16)
        grad_s_two = ((jnp.exp(logp_two) - codes_one) * grad_coef).astype(jnp.bfloat16)
        dz_one = jnp.einsum("nk,kd->nd", grad_s_one, protos, preferred_element_type=jnp.float32)
        dz_two = jnp.einsum("nk,kd->nd", grad_s_two, protos, preferred_element_type=jnp.float32)
        proto_part = jnp.einsum("nk,nd->kd", grad_s_one, z_one, preferred_element_type=jnp.float32) + jnp.einsum("nk,nd->kd", grad_s_two, z_two, preferred_element_type=jnp.float32)
        grad_protos = lax.psum(proto_part, "data")
        return codes_one, codes_two, swap_loss, dz_one, dz_two, grad_protos

    row_spec = P("data", None)
    full_spec = P(None, None)
    return jax.shard_map(
        local_step,
        mesh=mesh,
        in_specs=(row_spec, row_spec, full_spec, row_spec, row_spec),
        out_specs=(row_spec, row_spec, P(), row_spec, row_spec, full_spec),
        check_vma=False,
    )
```

profile of v0, /device:TPU:1, one launch (start us, length us, event | category | flops | bytes accessed | tf_op | source)
XLA Modules:
  0.0 1216.9 jit_solution(3027751541909045832)
XLA Ops:
  7.2 12.4 %fusion.11 = (f32[8192]{0:T(1024)}, f32[576,8192]{1,0:T(8,128)}) fusion(bf16[8192,256]{1,0:T(8,128)(2,1)} %param.8, bf16[512,256]{1,0:T(8,128)(2,1)} %param.10, bf16[64,256]{1,0:T(8,128)(2,1)} %param.7), kind=kOutput, calls=%fused_computation.20 | convolution fusion | flops 2425937920 | bytes 23396352 | tf_op jit(solution)/shard_map/nd,kd->nk/dot_general | solution.py:13
  19.6 8.8 fusion.10
  30.4 2.1 exponential_reduce_fusion.1
  32.5 260.8 %all-reduce.14.cloned.1.call-done = (f32[8192]{0:T(1024)}, f32[8192]{0:T(1024)}) async-done(((f32[8192]{0:T(1024)}, f32[8192]{0:T(1024)}), (f32[8192]{0:T(1024)}, f32[8192]{0:T(1024)})) %all-reduce.14.cloned.1.call-update) | async-done | bytes 65552 | tf_op jit(solution)/shard_map/psum | solution.py:16
  294.1 9.6 divide_reduce_fusion
  303.7 11.9 fusion.7
  315.6 9.8 divide_reduce_fusion.1
  325.4 11.9 fusion.6
  339.2 258.6 %all-reduce.12.cloned.1.call-done = (f32[8192]{0:T(1024)}, f32[8192]{0:T(1024)}) async-done(((f32[8192]{0:T(1024)}, f32[8192]{0:T(1024)}), (f32[8192]{0:T(1024)}, f32[8192]{0:T(1024)})) %all-reduce.12.cloned.1.call-update) | async-done | bytes 65552 | tf_op jit(solution)/shard_map/psum | solution.py:16
  598.6 11.3 fusion.9
  610.0 10.5 fusion.8
  620.6 22.6 %fusion.26 = (f32[8192]{0:T(1024)}, f32[576,8192]{1,0:T(8,128)}, f32[8192]{0:T(1024)}, f32[576,8192]{1,0:T(8,128)}) fusion(f32[576]{0:T(1024)S(1)} %broadcast_multiply_fusion.6, f32[8192]{0:T(1024)S(1)} %broadcast_multiply_fusion.1, f32[576]{0:T(1024)S(1)} %broadcast_multiply_fusion.7, f32[8192]{0:T(1024)S(1)} %broadcast_multiply_fusion.2, ...), kind=kLoop, calls=%fused_computation.57 | loop fusion | flops 56606720 | bytes 75703296 | tf_op jit(solution)/shard_map/reduce_sum | solution.py:19
  643.5 2.1 exponential_reduce_fusion
  645.6 258.1 %all-reduce.10.cloned.1.call-done = (f32[8192]{0:T(1024)}, f32[8192]{0:T(1024)}) async-done(((f32[8192]{0:T(1024)}, f32[8192]{0:T(1024)}), (f32[8192]{0:T(1024)}, f32[8192]{0:T(1024)})) %all-reduce.10.cloned.1.call-update) | async-done | bytes 65552 | tf_op jit(solution)/shard_map/psum | solution.py:19
  906.3 4.3 multiply_convert_fusion.1
  913.9 4.3 multiply_convert_fusion
  918.2 4.7 convolution_add_fusion
  922.9 3.6 multiply_reduce_fusion
  926.5 3.6 multiply_reduce_fusion.1
  931.3 78.0 %psum.62 = f32[]{:T(128)} all-reduce(f32[]{:T(128)S(6)} %add.22), channel_id=1, replica_groups=mesh['data'=256] {'data'}, use_global_device_ids=true, to_apply=%region_22.0 | all-reduce | flops 1 | bytes 8 | tf_op jit(solution)/shard_map/psum | solution.py:36
  1009.9 3.6 fusion.30
  1013.6 3.6 fusion.31
  1017.2 184.3 %all-reduce.8.cloned.1.call-done = f32[8192,256]{1,0:T(8,128)} async-done(((f32[8192,256]{1,0:T(8,128)}), f32[8192,256]{1,0:T(8,128)}) %all-reduce.8.cloned.1.call-update) | async-done | bytes 8388624 | tf_op jit(solution)/shard_map/psum | solution.py:43
  1201.5 7.3 copy.18
  (50 shorter events, 11.7 us)
Async XLA Ops:
  7.2 12.4 %copy-start.2 = (bf16[64,256]{1,0:T(8,128)(2,1)S(1)}, bf16[64,256]{1,0:T(8,128)(2,1)}, u32[]{:S(2)}) copy-start(bf16[64,256]{1,0:T(8,128)(2,1)} %param.6) | copy-start | bytes 98308
  7.2 12.4 %copy-start.1 = (bf16[512,256]{1,0:T(8,128)(2,1)S(1)}, bf16[512,256]{1,0:T(8,128)(2,1)}, u32[]{:S(2)}) copy-start(bf16[512,256]{1,0:T(8,128)(2,1)} %param.9) | copy-start | bytes 786436
  7.2 286.2 %all-reduce.14.cloned.1.call-start = ((), (), s32[]{:S(2)}) async-start(), calls=%async_computation.3 | async-start | bytes 131072 | tf_op jit(solution)/shard_map/psum | solution.py:16
  7.2 12.4 %copy-start = (bf16[8192,256]{1,0:T(8,128)(2,1)S(1)}, bf16[8192,256]{1,0:T(8,128)(2,1)}, u32[]{:S(2)}) copy-start(bf16[8192,256]{1,0:T(8,128)(2,1)} %param.8) | copy-start | bytes 12582916
  28.4 569.4 %all-reduce.12.cloned.1.call-start = ((), (), s32[]{:S(2)}) async-start(), calls=%async_computation.2 | async-start | bytes 131072 | tf_op jit(solution)/shard_map/psum | solution.py:16
  303.7 11.9 copy-start.5
  337.3 566.4 %all-reduce.10.cloned.1.call-start = ((), (), s32[]{:S(2)}) async-start(), calls=%async_computation.1 | async-start | bytes 131072 | tf_op jit(solution)/shard_map/psum | solution.py:19
  598.6 11.4 copy-start.6
  598.6 21.9 %slice-start = ((s8[18874368]{0:T(1024)(128)(4,1)}), s8[4194304]{0:T(1024)(128)(4,1)S(1)}, s32[]{:S(2)}) async-start(s8[18874368]{0:T(1024)(128)(4,1)} %bitcast.10), calls=%async_computation.4 | async-start | bytes 8388608
  598.6 21.9 %slice-start.1 = ((s8[18874368]{0:T(1024)(128)(4,1)}), s8[4194304]{0:T(1024)(128)(4,1)S(1)}, s32[]{:S(2)}) async-start(s8[18874368]{0:T(1024)(128)(4,1)} %bitcast.10), calls=%async_computation.5 | async-start | bytes 8388608
  598.6 21.9 %slice-start.2 = ((s8[18874368]{0:T(1024)(128)(4,1)}), s8[4194304]{0:T(1024)(128)(4,1)S(1)}, s32[]{:S(2)}) async-start(s8[18874368]{0:T(1024)(128)(4,1)} %bitcast.10), calls=%async_computation.6 | async-start | bytes 8388608
  610.0 10.6 slice-start.3
  610.0 10.6 slice-start.4
  643.2 558.3 %all-reduce.8.cloned.1.call-start = ((), (), s32[]{:S(2)}) async-start(), calls=%async_computation | async-start | bytes 16777216 | tf_op jit(solution)/shard_map/psum | solution.py:43
  910.7 1.3 copy-start.4
  912.0 6.2 copy-start.3
Sparse Core Ops, SparseCore 0:
  28.5 264.7 all-reduce.13
  337.4 260.3 all-reduce.11
  643.3 260.3 all-reduce.9
  923.0 278.4 all-reduce.7
where the time goes:
time: 1220 us
  waiting for transfers between devices  962 us (79%)
  other arithmetic  117 us (10%)
  blocking collectives  78 us (6%)
  matrix products  34.3 us (3%)
  between operations  17.5 us (1%)
    psum x3, waiting for transfers between devices, view_codes(): col_sum = lax.psum(jnp.sum(transport, axis=0), 'data')  777 us
    psum x1, waiting for transfers between devices, local_step(): grad_protos = lax.psum(proto_part, 'data')  184 us
    psum x1, blocking collectives, local_step(): swap_loss = -lax.psum(part_loss, 'data') / (2 * batch_total)  78 us
    reduce_sum x3, other arithmetic, view_codes(): col_sum = lax.psum(jnp.sum(transport, axis=0), 'data')  46.5 us
    reduce_sum x4, other arithmetic, view_codes(): jnp.sum(transport, axis=1, keepdims=True)  41.1 us
  transfers between devices with their start and end apart: 4, of which 4 were waited for; matrix products, arithmetic and copies ran while one was open for 2% of the time, Pallas kernels for 0%

commit v1 on v0

v1 whole, which is shorter than its diff:
```python
import functools

import jax
import jax.numpy as jnp
from jax import lax
from jax.experimental import pallas as pl
from jax.experimental.pallas import tpu as pltpu
from jax.sharding import PartitionSpec as P

EPSILON = 0.05
TEMPERATURE = 0.1
ITERS = 3
CORES = 2
CHIPS_Z = 8
VMEM_LIMIT = 67043328
ROW_BLOCK = 192
LANES = 128
LOG2E = 1.4426950408889634
F32 = jnp.float32
MESH = pl.DeviceIdType.MESH


def dot_nt(a, b):
    return lax.dot_general(a, b, (((1,), (1,)), ((), ())), preferred_element_type=F32)


def sinkhorn_kernel(
    nz, plane, total_rows, protos_count,
    z_one, z_two, q_one, q_two, protos,
    scale_out,
    rows, cols, mat, wacc, rscale, csum, rs_buf, ex_buf, ag_buf,
    row_sem, col_sem, out_sem, rs_send, rs_recv, ex_send, ex_recv, ag_send, ag_recv,
):
    me = lax.axis_index("data")
    core = lax.rem(me, CORES)
    chip = lax.div(me, CORES)
    yx = lax.rem(chip, plane)
    zz = lax.div(chip, plane)
    members = nz * CORES
    mine = zz * CORES + core
    tiles = mat.shape[1]
    per = tiles // members
    n_rows = mat.shape[2]
    batch = z_one.shape[0]
    wide = per * LANES
    blocks = n_rows // ROW_BLOCK if n_rows % ROW_BLOCK == 0 else 1
    rb = n_rows // blocks

    def near(t):
        k, e = lax.div(t, 2), lax.rem(t, 2)
        j = lax.div(k + 1, 2)
        dz = j * (2 * lax.rem(k, 2) - 1)
        return lax.rem(zz + dz + nz, nz) * CORES + lax.rem(core + e, CORES)

    def member_dev(m):
        return (lax.div(m, CORES) * plane + yx) * CORES + lax.rem(m, CORES)

    def plane_dev(o):
        return (zz * plane + o) * CORES + core

    views = ((z_one, q_one), (z_two, q_two))
    row_copies = []
    for v, (z, q) in enumerate(views):
        row_copies.append([
            pltpu.make_async_copy(z, rows.at[v, pl.ds(0, batch)], row_sem.at[v, 0]),
            pltpu.make_async_copy(q, rows.at[v, pl.ds(batch, n_rows - batch)], row_sem.at[v, 1]),
        ])

    def col_copy(m):
        part = pl.ds(pl.multiple_of(m * wide, wide), wide)
        return pltpu.make_async_copy(protos.at[part], cols.at[part], col_sem.at[m])

    for c in row_copies[0]:
        c.start()

    def start_cols(t, carry):
        col_copy(near(members - 1 - t)).start()
        return carry

    lax.fori_loop(0, members, start_cols, 0)
    for c in row_copies[1]:
        c.start()

    barrier = pltpu.get_barrier_semaphore()

    def greet_members(t, carry):
        pl.semaphore_signal(barrier, inc=1, device_id=(member_dev(near(t)),), device_id_type=MESH)
        return carry

    def greet_plane(t, carry):
        pl.semaphore_signal(barrier, inc=1, device_id=(plane_dev(lax.rem(yx + t, plane)),), device_id_type=MESH)
        return carry

    lax.fori_loop(1, members, greet_members, 0)
    lax.fori_loop(1, plane, greet_plane, 0)

    def rs_copy(it, v, m):
        return pltpu.make_async_remote_copy(
            src_ref=csum.at[it, v, m], dst_ref=rs_buf.at[it, v, mine],
            send_sem=rs_send.at[it, v], recv_sem=rs_recv.at[it, v],
            device_id=(member_dev(m),), device_id_type=MESH)

    def rs_start(it, v, t):
        rs_copy(it, v, near(members - 1 - t)).start()

    def rs_start_all(it, v):
        def send(t, carry):
            rs_start(it, v, t)
            return carry
        lax.fori_loop(0, members - 1, send, 0)

    def first_pass(v):
        for c in row_copies[v]:
            c.wait()

        def step(t, carry):
            m = near(members - 1 - t)
            if v == 0:
                col_copy(m).wait()
            part = pl.ds(pl.multiple_of(m * wide, wide), wide)
            scores = dot_nt(rows[v], cols[part, :])
            for j in range(per):
                e = jnp.exp2(scores[:, j * LANES:(j + 1) * LANES] * (LOG2E / EPSILON))
                mat[v, m * per + j] = e
                csum[0, v, m, pl.ds(j, 1), :] = jnp.sum(e, axis=0, keepdims=True)
            return carry

        lax.fori_loop(0, members, step, 0)

    first_pass(0)
    pl.semaphore_wait(barrier, members + plane - 2)
    rs_start_all(0, 0)
    first_pass(1)
    rs_start_all(0, 1)

    def wait_bytes(ref, sem):
        pltpu.make_async_copy(ref, ref, sem).wait()

    def reduce_slice(it, v):
        wait_bytes(rs_buf.at[it, v, pl.ds(0, members - 1)], rs_recv.at[it, v])
        rs_buf[it, v, mine] = csum[it, v, mine]
        ex_buf[it, v, yx] = jnp.sum(rs_buf[it, v], axis=0)

        def send(t, carry):
            o = lax.rem(yx + t, plane)
            pltpu.make_async_remote_copy(
                src_ref=ex_buf.at[it, v, yx], dst_ref=ex_buf.at[it, v, yx],
                send_sem=ex_send.at[it, v], recv_sem=ex_recv.at[it, v],
                device_id=(plane_dev(o),), device_id_type=MESH).start()
            return carry

        lax.fori_loop(1, plane, send, 0)

    def share_scale(it, v):
        wait_bytes(ex_buf.at[it, v, pl.ds(0, plane - 1)], ex_recv.at[it, v])
        ag_buf[it, v, mine] = 1.0 / (protos_count * jnp.sum(ex_buf[it, v], axis=0))

        def send(t, carry):
            m = near(members - t)
            pltpu.make_async_remote_copy(
                src_ref=ag_buf.at[it, v, mine], dst_ref=ag_buf.at[it, v, mine],
                send_sem=ag_send.at[it, v], recv_sem=ag_recv.at[it, v, mine],
                device_id=(member_dev(m),), device_id_type=MESH).start()
            return carry

        lax.fori_loop(1, members, send, 0)

    def all_reduce(it):
        for v in range(2):
            reduce_slice(it, v)
        for v in range(2):
            share_scale(it, v)

    def wait_scale(it, v, m):
        wait_bytes(ag_buf.at[it, v, m], ag_recv.at[it, v, m])

    def next_pass(it, v):
        wacc[...] = jnp.zeros_like(wacc)

        def add_slice(t, carry):
            m = near(t)

            @pl.when(t > 0)
            def _():
                wait_scale(it, v, m)

            for b in range(blocks):
                part = pl.ds(b * rb, rb)
                acc = wacc[part, :]
                for j in range(per):
                    acc += mat[v, m * per + j, part, :] * ag_buf[it, v, m, pl.ds(j, 1), :]
                wacc[part, :] = acc
            return carry

        lax.fori_loop(0, members, add_slice, 0)
        row_sum = jnp.sum(wacc[...], axis=1, keepdims=True)
        rscale[...] = jnp.broadcast_to(1.0 / (total_rows * row_sum), rscale.shape)

        def col_slice(t, carry):
            m = near(members - 1 - t)
            acc = [None] * per
            for b in range(blocks):
                part = pl.ds(b * rb, rb)
                r = rscale[part, :]
                for j in range(per):
                    p = (mat[v, m * per + j, part, :] * r).reshape(rb // 8, 8, LANES).sum(axis=0)
                    acc[j] = p if acc[j] is None else acc[j] + p
            for j in range(per):
                csum[it + 1, v, m, pl.ds(j, 1), :] = jnp.sum(acc[j], axis=0, keepdims=True)

            @pl.when(t > 0)
            def _():
                rs_start(it + 1, v, t - 1)
            return carry

        lax.fori_loop(0, members, col_slice, 0)

    def iteration(it, carry):
        all_reduce(it)
        for v in range(2):
            next_pass(it, v)
        return carry

    lax.fori_loop(0, ITERS - 1, iteration, 0)
    last = ITERS - 1
    all_reduce(last)
    outs = []
    for v in range(2):
        def wait_one(t, carry):
            wait_scale(last, v, near(t))
            return carry
        lax.fori_loop(1, members, wait_one, 0)
        outs.append(pltpu.make_async_copy(ag_buf.at[last, v], scale_out.at[v], out_sem.at[v]))
        outs[v].start()

    def drain(it, carry):
        for v in range(2):
            wait_bytes(rs_buf.at[it, v, pl.ds(0, members - 1)], rs_send.at[it, v])
            wait_bytes(ex_buf.at[it, v, pl.ds(0, plane - 1)], ex_send.at[it, v])
            wait_bytes(rs_buf.at[it, v, pl.ds(0, members - 1)], ag_send.at[it, v])
        return carry

    lax.fori_loop(0, ITERS, drain, 0)
    for c in outs:
        c.wait()


def column_scales(nz, plane, z_one, z_two, q_one, q_two, protos):
    batch, dim = z_one.shape
    n_rows = batch + q_one.shape[0]
    count = protos.shape[0]
    tiles = count // LANES
    members = nz * CORES
    per = tiles // members
    total_rows = nz * plane * CORES * n_rows
    any_spec = pl.BlockSpec(memory_space=pl.ANY)
    small = (per, LANES)
    dma = pltpu.SemaphoreType.DMA
    scales = pl.pallas_call(
        functools.partial(sinkhorn_kernel, nz, plane, float(total_rows), float(count)),
        out_shape=jax.ShapeDtypeStruct((2, members) + small, F32),
        in_specs=[any_spec] * 5,
        out_specs=any_spec,
        scratch_shapes=[
            pltpu.VMEM((2, n_rows, dim), jnp.bfloat16),
            pltpu.VMEM((count, dim), jnp.bfloat16),
            pltpu.VMEM((2, tiles, n_rows, LANES), F32),
            pltpu.VMEM((n_rows, LANES), F32),
            pltpu.VMEM((n_rows, LANES), F32),
            pltpu.VMEM((ITERS, 2, members) + small, F32),
            pltpu.VMEM((ITERS, 2, members) + small, F32),
            pltpu.VMEM((ITERS, 2, plane) + small, F32),
            pltpu.VMEM((ITERS, 2, members) + small, F32),
            dma((2, 2)),
            dma((members,)),
            dma((2,)),
            dma((ITERS, 2)),
            dma((ITERS, 2)),
            dma((ITERS, 2)),
            dma((ITERS, 2)),
            dma((ITERS, 2)),
            dma((ITERS, 2, members)),
        ],
        compiler_params=pltpu.CompilerParams(
            collective_id=0, has_side_effects=True, vmem_limit_bytes=VMEM_LIMIT),
        name="sinkhorn",
    )(z_one, z_two, q_one, q_two, protos)
    return scales.reshape(2, count)


def solution(mesh, nz=CHIPS_Z):
    group_size = mesh.shape["data"]
    plane = group_size // (nz * CORES)

    def local_step(z_one, z_two, protos, queue_one, queue_two):
        batch_rows = z_one.shape[0]
        batch_total = group_size * batch_rows
        scales = column_scales(nz, plane, z_one, z_two, queue_one, queue_two, protos)

        def codes_of(z, scale):
            score = dot_nt(z, protos)
            plan = jnp.exp(score / EPSILON) * scale
            return plan / jnp.sum(plan, axis=1, keepdims=True), score

        codes_one, score_one = codes_of(z_one, scales[0])
        codes_two, score_two = codes_of(z_two, scales[1])
        logp_one = jax.nn.log_softmax(score_one / TEMPERATURE, axis=1)
        logp_two = jax.nn.log_softmax(score_two / TEMPERATURE, axis=1)
        part_loss = jnp.sum(codes_two * logp_one) + jnp.sum(codes_one * logp_two)
        swap_loss = -lax.psum(part_loss, "data") / (2 * batch_total)
        grad_coef = 1.0 / (2 * batch_total * TEMPERATURE)
        grad_s_one = ((jnp.exp(logp_one) - codes_two) * grad_coef).astype(jnp.bfloat16)
        grad_s_two = ((jnp.exp(logp_two) - codes_one) * grad_coef).astype(jnp.bfloat16)
        dz_one = jnp.dot(grad_s_one, protos, preferred_element_type=F32)
        dz_two = jnp.dot(grad_s_two, protos, preferred_element_type=F32)
        proto_part = (jnp.einsum("nk,nd->kd", grad_s_one, z_one, preferred_element_type=F32)
                      + jnp.einsum("nk,nd->kd", grad_s_two, z_two, preferred_element_type=F32))
        grad_protos = lax.psum(proto_part, "data")
        return codes_one, codes_two, swap_loss, dz_one, dz_two, grad_protos

    row_spec = P("data", None)
    full_spec = P(None, None)
    return jax.shard_map(
        local_step,
        mesh=mesh,
        in_specs=(row_spec, row_spec, full_spec, row_spec, row_spec),
        out_specs=(row_spec, row_spec, P(), row_spec, row_spec, full_spec),
        check_vma=False,
    )
```

time: 1220 us -> 389 us (0.32)
  waiting for transfers between devices: 962 us -> 190 us
  other arithmetic: 117 us -> 10.7 us
  Pallas kernels: 0 us -> 66.9 us
  matrix products: 34.3 us -> 20.5 us
    psum x3 -> x0, waiting for transfers between devices: 777 us -> none  [view_codes(): col_sum = lax.psum(jnp.sum(transport, axis=0), 'data')]
    reduce_sum x11 -> x2, other arithmetic: 95.5 us -> 3.05 us  [the longest x1 2.53 us: local_step(): logp_one = jax.nn.log_softmax(score_one / TEMPERATURE, axis=1)]
    pallas_call x0 -> x1, Pallas kernels: none -> 66.9 us  [column_scales(): pl.pallas_call(functools.partial(sinkhorn_kernel, nz, plane, float(total_...]
    dot_general x6, matrix products: 34.3 us -> 20.5 us  [the longest x2 9.03 us: dot_nt(): lax.dot_general(a, b, (((1,), (1,)), ((), ())), preferred_element_type=F32)]
  transfers between devices with their start and end apart: 4 -> 1, of which waited for: 4 -> 1; matrix products, arithmetic and copies ran while one was open for 2% -> 2% of each run, Pallas kernels for 0% -> 0%
where the time goes in v1:
time: 389 us; the launch traced here: 388 us
  waiting for transfers between devices  190 us (49%)
  blocking collectives  74.7 us (19%)
  Pallas kernels  66.9 us (17%)
  matrix products  20.5 us (5%)
  between operations  17.3 us (4%)
  other arithmetic  10.7 us (3%)
  local copies, waits for them, and re-layouts  8.32 us (2%)
    psum x1, waiting for transfers between devices, local_step(): grad_protos = lax.psum(proto_part, 'data')  190 us
    psum x1, blocking collectives, local_step(): swap_loss = -lax.psum(part_loss, 'data') / (2 * batch_total)  74.7 us
    pallas_call x1, Pallas kernels, column_scales(): pl.pallas_call(functools.partial(sinkhorn_kernel, nz, plane, float(total_...  66.9 us
    dot_general x2, matrix products, dot_nt(): lax.dot_general(a, b, (((1,), (1,)), ((), ())), preferred_element_type=F32)  9.03 us
  transfers between devices with their start and end apart: 1, of which 1 were waited for; matrix products, arithmetic and copies ran while one was open for 2% of the time, Pallas kernels for 0%

profile of v1, /device:TPU:1, one launch (start us, length us, event | category | flops | bytes accessed | tf_op | source)
XLA Modules:
  0.0 388.4 jit_solution(7662559825734476847)
XLA Ops:
  7.2 0.0 copy-start.7
  7.2 0.0 all-reduce.2.cloned.1.call-start
  7.2 0.0 copy-start
  7.2 5.7 %multiply_reduce_fusion.3 = (f32[64]{0:T(128)}, f32[64,8192]{1,0:T(8,128)}) fusion(bf16[64,256]{1,0:T(8,128)(2,1)} %z_one.1, bf16[8192,256]{1,0:T(8,128)(2,1)} %protos.1), kind=kOutput, calls=%fused_computation.11 | convolution fusion | flops 269483968 | bytes 6324480 | tf_op jit(solution)/shard_map/dot_general | solution.py:24
  12.9 3.3 multiply_reduce_fusion.2
  16.3 66.9 %sinkhorn.1 = f32[2,16,4,128]{3,2,1,0:T(4,128)} custom-call(bf16[64,256]{1,0:T(8,128)(2,1)} %z_one.1, bf16[64,256]{1,0:T(8,128)(2,1)} %z_two.1, bf16[512,256]{1,0:T(8,128)(2,1)} %q_one.1, bf16[512,256]{1,0:T(8,128)(2,1)} %q_two.1, bf16[8192,256]{1,0:T(8,128)(2,1)} %protos.1), custom_call_target="tpu_custom_call" | custom-call | tf_op jit(solution)/shard_map/sinkhorn/pallas_call | solution.py:259
  83.2 0.0 copy-start.3
  83.2 0.0 copy-start.10
  83.2 0.9 fusion.6
  84.1 2.5 exponential_reduce_fusion.1
  86.7 0.5 exponential_reduce_fusion
  87.2 0.9 multiply_convert_fusion
  88.2 0.0 copy-start.9
  88.2 1.6 multiply_reduce_fusion
  89.8 2.2 multiply_convert_fusion.1
  92.0 1.3 fusion.9
  93.3 4.7 %convolution_add_fusion = f32[8192,256]{1,0:T(8,128)} fusion(f32[8192,256]{1,0:T(8,128)S(1)} %fusion.9, bf16[64,8192]{1,0:T(8,128)(2,1)S(1)} %get-tuple-element.11, bf16[64,256]{1,0:T(8,128)(2,1)S(1)} %copy-done.8), kind=kOutput, calls=%fused_computation | convolution fusion | flops 270532608 | bytes 17858560 | tf_op jit(solution)/shard_map/nk,nd->kd/dot_general | solution.py:317
  98.0 0.0 all-reduce.2.cloned.1.call-update
  98.1 2.9 multiply_reduce_fusion.1
  102.3 74.7 %psum.14 = f32[]{:T(128)} all-reduce(f32[]{:T(128)S(6)} %add.10), channel_id=1, replica_groups=mesh['data'=256] {'data'}, use_global_device_ids=true, to_apply=%region_6.0 | all-reduce | flops 1 | bytes 8 | tf_op jit(solution)/shard_map/psum | solution.py:310
  177.7 4.1 %fusion.8 = f32[64,256]{1,0:T(8,128)} fusion(bf16[64,8192]{1,0:T(8,128)(2,1)} %copy-done.4, bf16[8192,256]{1,0:T(8,128)(2,1)} %protos.1), kind=kOutput, calls=%fused_computation.19 | convolution fusion | flops 268435456 | bytes 5308416 | tf_op jit(solution)/shard_map/dot_general | solution.py:315
  181.8 1.4 fusion.7
  183.2 189.9 %all-reduce.2.cloned.1.call-done = f32[8192,256]{1,0:T(8,128)} async-done(((f32[8192,256]{1,0:T(8,128)}), f32[8192,256]{1,0:T(8,128)}) %all-reduce.2.cloned.1.call-update) | async-done | bytes 8388624 | tf_op jit(solution)/shard_map/psum | solution.py:318
  373.1 7.3 %copy.12 = f32[8192,256]{1,0:T(8,128)} copy(f32[8192,256]{1,0:T(8,128)} %all-reduce.2.cloned.1.call-done) | data formatting | bytes 16777216
  (19 shorter events, 0.1 us)
Async XLA Ops:
  7.2 5.8 %copy-start.7 = (bf16[64,256]{1,0:T(8,128)(2,1)S(1)}, bf16[64,256]{1,0:T(8,128)(2,1)}, u32[]{:S(2)}) copy-start(bf16[64,256]{1,0:T(8,128)(2,1)} %z_two.1) | copy-start | bytes 98308
  7.2 365.9 %all-reduce.2.cloned.1.call-start = ((), (), s32[]{:S(2)}) async-start(), calls=%async_computation | async-start | bytes 16777216 | tf_op jit(solution)/shard_map/psum | solution.py:318
  7.2 5.7 %copy-start = (bf16[8192,256]{1,0:T(8,128)(2,1)S(1)}, bf16[8192,256]{1,0:T(8,128)(2,1)}, u32[]{:S(2)}) copy-start(bf16[8192,256]{1,0:T(8,128)(2,1)} %protos.1) | copy-start | bytes 12582916
  83.2 3.5 copy-start.3
  83.2 3.5 copy-start.10
  84.1 3.1 copy-start.2
  88.1 1.7 copy-start.5
  88.1 5.2 %copy-start.4 = (bf16[64,8192]{1,0:T(8,128)(2,1)}, bf16[64,8192]{1,0:T(8,128)(2,1)S(1)}, u32[]{:S(2)}) copy-start(bf16[64,8192]{1,0:T(8,128)(2,1)S(1)} %get-tuple-element.11) | copy-start | bytes 3145732
  88.2 1.6 copy-start.9
  89.8 2.2 copy-start.6
  92.0 1.3 copy-start.8
  177.7 4.1 %copy-start.1 = (bf16[8192,256]{1,0:T(8,128)(2,1)S(1)}, bf16[8192,256]{1,0:T(8,128)(2,1)}, u32[]{:S(2)}) copy-start(bf16[8192,256]{1,0:T(8,128)(2,1)} %protos.1) | copy-start | bytes 12582916
Sparse Core Ops, SparseCore 0:
  98.2 274.8 all-reduce.1

commit v2 on v1

--- a/solution.py
+++ b/solution.py
@@ -12,6 +12,7 @@
 ITERS = 3
 CORES = 2
 CHIPS_Z = 8
+CHIPS_X = 4
 VMEM_LIMIT = 67043328
 ROW_BLOCK = 192
 LANES = 128
@@ -288,34 +289,410 @@
     return scales.reshape(2, count)
 
 
-def solution(mesh, nz=CHIPS_Z):
+def codes_kernel(
+    grad_coef, z_one, z_two, protos, scale_refs,
+    codes_one, codes_two, grad_out, dz_one, dz_two, loss_out,
+    cols, score, plan, prob, col_sem, out_sem,
+):
+    chunks, batch, wide = score.shape[1:]
+    rows = (z_one, z_two)
+    scales = scale_refs
+
+    def col_copy(t):
+        part = pl.ds(pl.multiple_of(t * wide, wide), wide)
+        return pltpu.make_async_copy(protos.at[part], cols.at[part], col_sem.at[t])
+
+    def start(t, carry):
+        col_copy(t).start()
+        return carry
+
+    lax.fori_loop(0, chunks, start, 0)
+    zero = jnp.zeros((batch, LANES), F32)
+    per = wide // LANES
+
+    def lane_fold(x):
+        return sum(x[:, j * LANES:(j + 1) * LANES] for j in range(per))
+
+    def scan(t, carry):
+        col_copy(t).wait()
+        part = pl.ds(pl.multiple_of(t * wide, wide), wide)
+        sums = []
+        for v in range(2):
+            s = dot_nt(rows[v][...], cols[part, :])
+            score[v, t] = s
+            b = jnp.exp2(s * (LOG2E / TEMPERATURE))
+            prob[v, t] = b
+            a = jnp.exp2(s * (LOG2E / EPSILON)) * scales[v, pl.ds(t, 1), :]
+            plan[v, t] = a
+            sums += [carry[2 * v] + lane_fold(a), carry[2 * v + 1] + lane_fold(b)]
+        return tuple(sums)
+
+    sums = lax.fori_loop(0, chunks, scan, (zero,) * 4)
+    row_sum = [jnp.sum(x, axis=1, keepdims=True) for x in sums]
+    inv = [1.0 / x for x in row_sum]
+    lse = [jnp.log(row_sum[2 * v + 1]) for v in range(2)]
+
+    def code_copy(v, t):
+        out = (codes_one, codes_two)[v]
+        return pltpu.make_async_copy(
+            plan.at[v, t], out.at[:, pl.ds(pl.multiple_of(t * wide, wide), wide)], out_sem.at[v])
+
+    def finish(t, carry):
+        loss, dz = carry
+        part = pl.ds(pl.multiple_of(t * wide, wide), wide)
+        codes = [plan[v, t] * inv[2 * v] for v in range(2)]
+        for v in range(2):
+            plan[v, t] = codes[v]
+        grads = []
+        for v in range(2):
+            p = prob[v, t] * inv[2 * v + 1]
+            other = codes[1 - v]
+            grads.append(((p - other) * grad_coef).astype(jnp.bfloat16))
+            loss = loss + lane_fold(other * (score[v, t] * (1.0 / TEMPERATURE) - lse[v]))
+        both = jnp.concatenate(grads, axis=0)
+        grad_out[t] = both
+        dz = dz + jnp.dot(both, cols[part, :], preferred_element_type=F32)
+        for v in range(2):
+            code_copy(v, t).start()
+        return loss, dz
+
+    loss, dz = lax.fori_loop(
+        0, chunks, finish, (zero, jnp.zeros((2 * batch, cols.shape[1]), F32)))
+    dz_one[...] = dz[:batch]
+    dz_two[...] = dz[batch:]
+    loss_out[...] = jnp.sum(loss, axis=0, keepdims=True)
+
+    def drain(t, carry):
+        for v in range(2):
+            code_copy(v, t).wait()
+        return carry
+
+    lax.fori_loop(0, chunks, drain, 0)
+
+
+def batch_codes(chunks, grad_coef, z_one, z_two, protos, scales):
+    batch, dim = z_one.shape
+    count = protos.shape[0]
+    wide = count // chunks
+    any_spec = pl.BlockSpec(memory_space=pl.ANY)
+    vmem = pl.BlockSpec(memory_space=pltpu.VMEM)
+    big = pltpu.VMEM((2, chunks, batch, wide), F32)
+    return pl.pallas_call(
+        functools.partial(codes_kernel, grad_coef),
+        out_shape=(
+            jax.ShapeDtypeStruct((batch, count), F32),
+            jax.ShapeDtypeStruct((batch, count), F32),
+            jax.ShapeDtypeStruct((chunks, 2 * batch, wide), jnp.bfloat16),
+            jax.ShapeDtypeStruct((batch, dim), F32),
+            jax.ShapeDtypeStruct((batch, dim), F32),
+            jax.ShapeDtypeStruct((1, LANES), F32),
+        ),
+        in_specs=[vmem, vmem, any_spec, vmem],
+        out_specs=(any_spec, any_spec, vmem, vmem, vmem, vmem),
+        scratch_shapes=[
+            pltpu.VMEM((count, dim), jnp.bfloat16), big, big, big,
+            pltpu.SemaphoreType.DMA((chunks,)), pltpu.SemaphoreType.DMA((2,)),
+        ],
+        compiler_params=pltpu.CompilerParams(vmem_limit_bytes=48 * 2 ** 20),
+        name="codes",
+    )(z_one, z_two, protos, scales.reshape(2, chunks, wide))
+
+
+def protos_kernel(
+    nz, ny, nx,
+    grads, z_rows, loss_in,
+    total, loss_out,
+    g_buf, z_buf, part_buf, y_buf, yz_buf, sums, loss_buf,
+    own_sem, z_send, z_recv, g_send, g_recv, p_send, p_recv, s_send, s_recv,
+    az_send, az_recv, ay_send, ay_recv, ax_send, ax_recv, af_send, af_recv, pair_send, pair_recv,
+    out_sem, l_send, l_recv,
+):
+    me = lax.axis_index("data")
+    core = lax.rem(me, CORES)
+    chip = lax.div(me, CORES)
+    x = lax.rem(chip, nx)
+    y = lax.rem(lax.div(chip, nx), ny)
+    z = lax.div(chip, nx * ny)
+    halves = 2
+
+    def dev(xx, yy, z2, cc):
+        return ((z2 * ny + yy) * nx + xx) * CORES + cc
+
+    def remote(src, dst, send, recv, device):
+        return pltpu.make_async_remote_copy(
+            src_ref=src, dst_ref=dst, send_sem=send, recv_sem=recv, device_id=(device,), device_id_type=MESH)
+
+    def wait_bytes(ref, sem):
+        pltpu.make_async_copy(ref, ref, sem).wait()
+
+    n_first, n_second = (nx, ny), (ny, nx)
+    first, second = (x, y), (y, x)
+
+    def dev_first(col, f, cc):
+        return dev(f, y, z, cc) if col == 0 else dev(x, f, z, cc)
+
+    def dev_second(col, s):
+        return dev(x, s, z, core) if col == 0 else dev(s, y, z, core)
+
+    members = [n_first[col] * CORES for col in range(2)]
+    slot = [first[col] * CORES + core for col in range(2)]
+
+    def member_dev(col, m):
+        return dev_first(col, lax.div(m, CORES), lax.rem(m, CORES))
+
+    barrier = pltpu.get_barrier_semaphore()
+    greeted = 0
+    for col in range(2):
+        for t in range(1, members[col]):
+            if col == 1 and t == 1:
+                continue
+            f = lax.rem(first[col] + t // CORES, n_first[col])
+            cc = lax.rem(core + t % CORES, CORES)
+            pl.semaphore_signal(barrier, inc=1, device_id=(dev_first(col, f, cc),), device_id_type=MESH)
+            greeted += 1
+    for t in range(1, nz):
+        pl.semaphore_signal(barrier, inc=1, device_id=(dev(x, y, lax.rem(z + t, nz), core),), device_id_type=MESH)
+        greeted += 1
+
+    own_z = pltpu.make_async_copy(z_rows, z_buf.at[0, slot[0]], own_sem.at[0])
+    own_z2 = pltpu.make_async_copy(z_rows, z_buf.at[1, slot[1]], own_sem.at[1])
+    own_l = pltpu.make_async_copy(loss_in, loss_buf.at[0, slot[0]], own_sem.at[2])
+    own_z.start()
+    own_z2.start()
+    own_l.start()
+    own_z.wait()
+    own_z2.wait()
+    own_l.wait()
+    pl.semaphore_wait(barrier, greeted)
+
+    width = part_buf.shape[2]
+    order = [(h, col) for h in range(halves) for col in range(2)]
+
+    def far(n, t):
+        offs = sorted(range(1, n), key=lambda d: -min(d, n - d))
+        return offs[t]
+
+    def group_offsets(col):
+        n = n_first[col]
+        offs = [(far(n, t), c) for t in range(n - 1) for c in range(CORES)]
+        return offs + [(0, 1)]
+
+    for col in range(2):
+        for df, dc in group_offsets(col):
+            f = lax.rem(first[col] + df, n_first[col])
+            cc = lax.rem(core + dc, CORES)
+            remote(z_buf.at[col, slot[col]], z_buf.at[col, slot[col]],
+                   z_send.at[col], z_recv.at[col], dev_first(col, f, cc)).start()
+    for h, col in order:
+        for df, dc in group_offsets(col):
+            f = lax.rem(first[col] + df, n_first[col])
+            cc = lax.rem(core + dc, CORES)
+            m = f * CORES + cc
+            block = (col * members[col] + m) * halves + h
+            remote(grads.at[block], g_buf.at[col, h, slot[col]],
+                   g_send.at[col, h], g_recv.at[col, h], dev_first(col, f, cc)).start()
+    for df, dc in group_offsets(0):
+        f = lax.rem(first[0] + df, n_first[0])
+        cc = lax.rem(core + dc, CORES)
+        remote(loss_buf.at[0, slot[0]], loss_buf.at[0, slot[0]], l_send.at[0], l_recv.at[0], dev_first(0, f, cc)).start()
+
+    own_copies = {}
+    for n, (h, col) in enumerate(order):
+        block = (col * members[col] + slot[col]) * halves + h
+        own_copies[h, col] = pltpu.make_async_copy(grads.at[block], g_buf.at[col, h, slot[col]], own_sem.at[3 + n])
+        own_copies[h, col].start()
+
+    block_rows = [width // n_second[col] for col in range(2)]
+    unit = block_rows[0] // nz
+
+    def address(col, h, f, cc, s, zi):
+        half_count = total.shape[0] // 2
+        return col * half_count + ((f * CORES + cc) * halves + h) * width + s * block_rows[col] + zi * unit
+
+    def stage_g(h, col):
+        own_copies[h, col].wait()
+        wait_bytes(g_buf.at[col, h, pl.ds(0, members[col] - 1)], g_recv.at[col, h])
+        if h == 0:
+            wait_bytes(z_buf.at[col, pl.ds(0, members[col] - 1)], z_recv.at[col])
+        k = members[col] * z_buf.shape[2]
+        g = g_buf[col, h].reshape(k, width)
+        zs = z_buf[col].reshape(k, z_buf.shape[3])
+        part_buf[col, h] = lax.dot_general(g, zs, (((0,), (0,)), ((), ())), preferred_element_type=F32)
+        for t in range(n_second[col] - 1):
+            s = lax.rem(second[col] + far(n_second[col], t), n_second[col])
+            rows = pl.ds(pl.multiple_of(s * block_rows[col], 8), block_rows[col])
+            remote(part_buf.at[col, h, rows], y_buf.at[col, h, second[col]],
+                   p_send.at[col, h], p_recv.at[col, h], dev_second(col, s)).start()
+
+    def stage_y(h, col):
+        n = n_second[col]
+        wait_bytes(y_buf.at[col, h, pl.ds(0, n - 1)], p_recv.at[col, h])
+        mine = pl.ds(pl.multiple_of(second[col] * block_rows[col], 8), block_rows[col])
+        y_buf[col, h, second[col]] = part_buf[col, h, mine]
+        yz_buf[col, h, 0] = jnp.sum(y_buf[col, h], axis=0)
+        for t in range(nz - 1):
+            z2 = lax.rem(z + far(nz, t), nz)
+            rows = pl.ds(pl.multiple_of(z2 * unit, 8), unit)
+            remote(yz_buf.at[col, h, 0, rows], sums.at[col, h, z],
+                   s_send.at[col, h], s_recv.at[col, h], dev(x, y, z2, core)).start()
+
+    def rows_of(addr, n):
+        return pl.ds(pl.multiple_of(addr, 8), n)
+
+    def stage_z(h, col):
+        wait_bytes(sums.at[col, h, pl.ds(0, nz - 1)], s_recv.at[col, h])
+        sums[col, h, z] = yz_buf[col, h, 0, pl.ds(pl.multiple_of(z * unit, 8), unit)]
+        own = rows_of(address(col, h, first[col], core, second[col], z), unit)
+        total[own, :] = jnp.sum(sums[col, h], axis=0)
+        for t in range(nz - 1):
+            z2 = lax.rem(z + far(nz, t), nz)
+            remote(total.at[own], total.at[own], az_send.at[col, h], az_recv.at[col, h], dev(x, y, z2, core)).start()
+
+    def stage_az(h, col):
+        n = n_second[col]
+        block = rows_of(address(col, h, first[col], core, second[col], 0), block_rows[col])
+        wait_bytes(total.at[pl.ds(0, (nz - 1) * unit)], az_recv.at[col, h])
+        for t in range(n - 1):
+            s = lax.rem(second[col] + far(n, t), n)
+            remote(total.at[block], total.at[block], ay_send.at[col, h], ay_recv.at[col, h], dev_second(col, s)).start()
+
+    def pair_send_block(h, col, k, rows):
+        remote(total.at[rows], total.at[rows], pair_send.at[col, h, k], pair_recv.at[col, h, k],
+               dev(x, y, z, 1 - core)).start()
+
+    def stage_ay(h, col):
+        n, n1 = n_second[col], n_first[col]
+        wait_bytes(total.at[pl.ds(0, (n - 1) * block_rows[col])], ay_recv.at[col, h])
+        whole = rows_of(address(col, h, first[col], core, 0, 0), width)
+        for d, step in enumerate((1, n1 - 1)):
+            f = lax.rem(first[col] + step, n1)
+            remote(total.at[whole], total.at[whole], ax_send.at[col, h, d], ax_recv.at[col, h, d],
+                   dev_first(col, f, core)).start()
+        pair_send_block(h, col, 0, whole)
+
+    def stage_ax(h, col):
+        n1 = n_first[col]
+        for d, step in enumerate((1, n1 - 1)):
+            src = lax.rem(first[col] + n1 - step, n1)
+            nxt = lax.rem(first[col] + step, n1)
+            whole = rows_of(address(col, h, src, core, 0, 0), width)
+            wait_bytes(total.at[whole], ax_recv.at[col, h, d])
+            part = rows_of(address(col, h, src, core, 0, 0) + d * (width // 2), width // 2)
+            remote(total.at[part], total.at[part], af_send.at[col, h, d], af_recv.at[col, h, d],
+                   dev_first(col, nxt, core)).start()
+            pair_send_block(h, col, 1 + d, whole)
+
+    def stage_af(h, col):
+        n1 = n_first[col]
+        src = lax.rem(first[col] + n1 // 2, n1)
+        for d in range(2):
+            part = rows_of(address(col, h, src, core, 0, 0) + d * (width // 2), width // 2)
+            wait_bytes(total.at[part], af_recv.at[col, h, d])
+            pair_send_block(h, col, 3 + d, part)
+
+    def loss_stage(k):
+        if k == 0:
+            wait_bytes(loss_buf.at[0, pl.ds(0, members[0] - 1)], l_recv.at[0])
+            loss_buf[1, y] = jnp.sum(loss_buf[0, pl.ds(0, members[0])], axis=0)
+            for t in range(1, ny):
+                remote(loss_buf.at[1, y], loss_buf.at[1, y], l_send.at[1], l_recv.at[1],
+                       dev(x, lax.rem(y + t, ny), z, core)).start()
+        elif k == 1:
+            wait_bytes(loss_buf.at[1, pl.ds(0, ny - 1)], l_recv.at[1])
+            loss_buf[2, z] = jnp.sum(loss_buf[1, pl.ds(0, ny)], axis=0)
+            for t in range(1, nz):
+                remote(loss_buf.at[2, z], loss_buf.at[2, z], l_send.at[2], l_recv.at[2],
+                       dev(x, y, lax.rem(z + t, nz), core)).start()
+        else:
+            wait_bytes(loss_buf.at[2, pl.ds(0, nz - 1)], l_recv.at[2])
+            loss_out[...] = jnp.sum(loss_buf[2, pl.ds(0, nz)], axis=0)
+
+    stages = [(stage_g, 0), (stage_y, 5), (stage_z, 10), (stage_az, 15), (stage_ay, 20), (stage_ax, 26), (stage_af, 30)]
+    plan = sorted(((at + 6 * h, k, h, col) for k, (_, at) in enumerate(stages) for h, col in order))
+    for _, k, h, col in plan:
+        stages[k][0](h, col)
+        if (h, col) == (1, 1) and k < 3:
+            loss_stage(k)
+
+    for h, col in order:
+        n1 = n_first[col]
+        for k, src, off, n in (
+            (0, first[col], 0, width),
+            (1, lax.rem(first[col] + n1 - 1, n1), 0, width),
+            (2, lax.rem(first[col] + 1, n1), 0, width),
+            (3, lax.rem(first[col] + n1 // 2, n1), 0, width // 2),
+            (4, lax.rem(first[col] + n1 // 2, n1), width // 2, width // 2),
+        ):
+            rows = rows_of(address(col, h, src, 1 - core, 0, 0) + off, n)
+            wait_bytes(total.at[rows], pair_recv.at[col, h, k])
+            wait_bytes(total.at[rows], pair_send.at[col, h, k])
+
+    for col in range(2):
+        wait_bytes(z_buf.at[col, pl.ds(0, members[col] - 1)], z_send.at[col])
+        for h in range(halves):
+            wait_bytes(g_buf.at[col, h, pl.ds(0, members[col] - 1)], g_send.at[col, h])
+            wait_bytes(y_buf.at[col, h, pl.ds(0, n_second[col] - 1)], p_send.at[col, h])
+            wait_bytes(sums.at[col, h, pl.ds(0, nz - 1)], s_send.at[col, h])
+            wait_bytes(total.at[pl.ds(0, (nz - 1) * unit)], az_send.at[col, h])
+            wait_bytes(total.at[pl.ds(0, (n_second[col] - 1) * block_rows[col])], ay_send.at[col, h])
+            for d in range(2):
+                wait_bytes(total.at[pl.ds(0, width)], ax_send.at[col, h, d])
+                wait_bytes(total.at[pl.ds(0, width // 2)], af_send.at[col, h, d])
+    wait_bytes(loss_buf.at[0, pl.ds(0, members[0] - 1)], l_send.at[0])
+    wait_bytes(loss_buf.at[1, pl.ds(0, ny - 1)], l_send.at[1])
+    wait_bytes(loss_buf.at[2, pl.ds(0, nz - 1)], l_send.at[2])
+
+
+def sum_protos(nz, ny, nx, grads, z_rows, loss):
+    blocks, rows, width = grads.shape
+    dim = z_rows.shape[1]
+    count = blocks * width
+    members = nx * CORES
+    any_spec = pl.BlockSpec(memory_space=pl.ANY)
+    vmem = pl.BlockSpec(memory_space=pltpu.VMEM)
+    dma = pltpu.SemaphoreType.DMA
+    two = dma((2, 2))
+    return pl.pallas_call(
+        functools.partial(protos_kernel, nz, ny, nx),
+        out_shape=(jax.ShapeDtypeStruct((count, dim), F32), jax.ShapeDtypeStruct((1, LANES), F32)),
+        in_specs=[any_spec, any_spec, any_spec],
+        out_specs=(vmem, vmem),
+        scratch_shapes=[
+            pltpu.VMEM((2, 2, members, rows, width), jnp.bfloat16),
+            pltpu.VMEM((2, members, rows, dim), jnp.bfloat16),
+            pltpu.VMEM((2, 2, width, dim), F32),
+            pltpu.VMEM((2, 2, ny, width // ny, dim), F32),
+            pltpu.VMEM((2, 2, 1, width // ny, dim), F32),
+            pltpu.VMEM((2, 2, nz, width // ny // nz, dim), F32),
+            pltpu.VMEM((3, max(members, nz), 1, LANES), F32),
+            dma((7,)),
+            dma((2,)), dma((2,)),
+            two, two, two, two, two, two, two, two, two, two,
+            dma((2, 2, 2)), dma((2, 2, 2)), dma((2, 2, 2)), dma((2, 2, 2)),
+            dma((2, 2, 5)), dma((2, 2, 5)),
+            dma((2,)),
+            dma((3,)), dma((3,)),
+        ],
+        compiler_params=pltpu.CompilerParams(
+            collective_id=1, has_side_effects=True, vmem_limit_bytes=48 * 2 ** 20),
+        name="protos",
+    )(grads, z_rows, loss)
+
+
+def solution(mesh, nz=CHIPS_Z, nx=CHIPS_X):
     group_size = mesh.shape["data"]
     plane = group_size // (nz * CORES)
+    ny = plane // nx
 
     def local_step(z_one, z_two, protos, queue_one, queue_two):
-        batch_rows = z_one.shape[0]
-        batch_total = group_size * batch_rows
+        batch_total = group_size * z_one.shape[0]
         scales = column_scales(nz, plane, z_one, z_two, queue_one, queue_two, protos)
-
-        def codes_of(z, scale):
-            score = dot_nt(z, protos)
-            plan = jnp.exp(score / EPSILON) * scale
-            return plan / jnp.sum(plan, axis=1, keepdims=True), score
-
-        codes_one, score_one = codes_of(z_one, scales[0])
-        codes_two, score_two = codes_of(z_two, scales[1])
-        logp_one = jax.nn.log_softmax(score_one / TEMPERATURE, axis=1)
-        logp_two = jax.nn.log_softmax(score_two / TEMPERATURE, axis=1)
-        part_loss = jnp.sum(codes_two * logp_one) + jnp.sum(codes_one * logp_two)
-        swap_loss = -lax.psum(part_loss, "data") / (2 * batch_total)
         grad_coef = 1.0 / (2 * batch_total * TEMPERATURE)
-        grad_s_one = ((jnp.exp(logp_one) - codes_two) * grad_coef).astype(jnp.bfloat16)
-        grad_s_two = ((jnp.exp(logp_two) - codes_one) * grad_coef).astype(jnp.bfloat16)
-        dz_one = jnp.dot(grad_s_one, protos, preferred_element_type=F32)
-        dz_two = jnp.dot(grad_s_two, protos, preferred_element_type=F32)
-        proto_part = (jnp.einsum("nk,nd->kd", grad_s_one, z_one, preferred_element_type=F32)
-                      + jnp.einsum("nk,nd->kd", grad_s_two, z_two, preferred_element_type=F32))
-        grad_protos = lax.psum(proto_part, "data")
+        codes_one, codes_two, grads, dz_one, dz_two, loss = batch_codes(
+            4 * nx * CORES, grad_coef, z_one, z_two, protos, scales)
+        z_rows = jnp.concatenate([z_one, z_two], axis=0)
+        grad_protos, loss = sum_protos(nz, ny, nx, grads, z_rows, loss)
+        swap_loss = -jnp.sum(loss) / (2 * batch_total)
         return codes_one, codes_two, swap_loss, dz_one, dz_two, grad_protos
 
     row_spec = P("data", None)

time: 389 us -> 167 us (0.43)
  waiting for transfers between devices: 190 us -> 0 us
  Pallas kernels: 66.9 us -> 153 us
  blocking collectives: 74.7 us -> 0 us
  matrix products: 20.5 us -> 0 us
  between operations: 17.3 us -> 2.44 us
  other arithmetic: 10.7 us -> 1.38 us
    psum x1 -> x0, waiting for transfers between devices: 190 us -> none  [local_step(): grad_protos = lax.psum(proto_part, 'data')]
    pallas_call x0 -> x2, Pallas kernels: none -> 86 us  [the longest x1 69.9 us: sum_protos(): pl.pallas_call(functools.partial(protos_kernel, nz, ny, nx), out_shape=(j...]
    psum x1 -> x0, blocking collectives: 74.7 us -> none  [local_step(): swap_loss = -lax.psum(part_loss, 'data') / (2 * batch_total)]
    dot_general x6 -> x0, matrix products: 20.5 us -> none  [the longest x2 9.03 us: dot_nt(): lax.dot_general(a, b, (((1,), (1,)), ((), ())), preferred_element_type=F32)]
    reduce_sum x4 -> x1, other arithmetic: 7.61 us -> 0.6 us  [local_step(): swap_loss = -jnp.sum(loss) / (2 * batch_total)]
    unnamed x23 -> x5, local copies, waits for them, and re-layouts: 7.38 us -> 8.83 us
  transfers between devices with their start and end apart: 1 -> 0, of which waited for: 1 -> 0; matrix products, arithmetic and copies ran while one was open for 2% -> 0% of each run, Pallas kernels for 0% -> 0%
where the time goes in v2:
time: 167 us; the launch traced here: 166 us
  Pallas kernels  153 us (92%)
  local copies, waits for them, and re-layouts  9.71 us (6%)
  between operations  2.44 us (1%)
    pallas_call x1, Pallas kernels, sum_protos(): pl.pallas_call(functools.partial(protos_kernel, nz, ny, nx), out_shape=(j...  69.9 us
    pallas_call x1, Pallas kernels, column_scales(): pl.pallas_call(functools.partial(sinkhorn_kernel, nz, plane, float(total_...  66.9 us
    pallas_call x1, Pallas kernels, batch_codes(): pl.pallas_call(functools.partial(codes_kernel, grad_coef), out_shape=(jax...  16.1 us
    unnamed x5, local copies, waits for them, and re-layouts  8.83 us

profile of v2, /device:TPU:1, one launch (start us, length us, event | category | flops | bytes accessed | tf_op | source)
XLA Modules:
  0.0 166.4 jit_solution(16483068581933552738)
XLA Ops:
  0.6 66.9 %sinkhorn.1 = f32[2,16,4,128]{3,2,1,0:T(4,128)} custom-call(bf16[64,256]{1,0:T(8,128)(2,1)} %z_one.3, bf16[64,256]{1,0:T(8,128)(2,1)} %z_two.3, bf16[512,256]{1,0:T(8,128)(2,1)} %q_one.1, bf16[512,256]{1,0:T(8,128)(2,1)} %q_two.1, bf16[8192,256]{1,0:T(8,128)(2,1)} %protos.4), custom_call_target="tpu_custom_call" | custom-call | tf_op jit(solution)/shard_map/sinkhorn/pallas_call | solution.py:260
  67.5 0.9 reshape_reshape.3.scale_refs
  68.4 0.8 pad_maximum_fusion.z_rows
  69.2 0.0 copy-start
  69.2 0.8 copy-done
  69.9 0.0 copy-start.1
  69.9 0.8 copy-done.1
  70.7 16.1 %codes.1 = (f32[64,8192]{1,0:T(8,128)}, f32[64,8192]{1,0:T(8,128)}, bf16[32,128,256]{2,1,0:T(8,128)(2,1)S(1)}, f32[64,256]{1,0:T(8,128)}, f32[64,256]{1,0:T(8,128)}, /*index=5*/f32[1,128]{1,0:T(1,128)S(1)}) custom-call(bf16[64,256]{1,0:T(8,128)(2,1)S(1)} %copy-done, bf16[64,256]{1,0:T(8,128)(2,1)S(1)} %copy-done.1, bf16[8192,256]{1,0:T(8,128)(2,1)} %protos.4, ...), custom_call_target="tpu_custom_call" | custom-call | tf_op jit(solution)/shard_map/codes/pallas_call | solution.py:380
  86.8 69.9 %protos.5 = (f32[8192,256]{1,0:T(8,128)}, f32[1,128]{1,0:T(1,128)S(1)}) custom-call(bf16[32,128,256]{2,1,0:T(8,128)(2,1)S(1)} %get-tuple-element.16.grads, bf16[128,256]{1,0:T(8,128)(2,1)S(1)} %pad_maximum_fusion.z_rows, f32[1,128]{1,0:T(1,128)S(1)} %get-tuple-element.17.loss_in), custom_call_target="tpu_custom_call" | custom-call | tf_op jit(solution)/shard_map/protos/pallas_call | solution.py:655
  156.7 0.6 reduce_sum.9
  157.9 7.3 %copy.12 = f32[8192,256]{1,0:T(8,128)} copy(f32[8192,256]{1,0:T(8,128)} %get-tuple-element.33) | data formatting | bytes 16777216
Async XLA Ops:
  69.2 0.8 copy-start
  69.9 0.8 copy-start.1

commit v3 on v1

v3 whole, which is shorter than its diff:
```python
import functools

import jax
import jax.numpy as jnp
from jax import lax
from jax.experimental import pallas as pl
from jax.experimental.pallas import tpu as pltpu
from jax.sharding import PartitionSpec as P

EPSILON = 0.05
TEMPERATURE = 0.1
ITERS = 3
CORES = 2
CHIPS_Z = 8
CHIPS_X = 4
VMEM_TOTAL = 67043328
LANES = 128
HALVES = 2
LOG2E = 1.4426950408889634
F32 = jnp.float32
BF16 = jnp.bfloat16
MESH = pl.DeviceIdType.MESH


def dot_nt(a, b):
    return lax.dot_general(a, b, (((1,), (1,)), ((), ())), preferred_element_type=F32)


def near_offset(k):
    return lax.div(k + 1, 2) * (2 * lax.rem(k, 2) - 1)


def far_first(n):
    return sorted(range(1, n), key=lambda d: (-min(d, n - d), d))


def remote(src, dst, send, recv, device):
    return pltpu.make_async_remote_copy(
        src_ref=src, dst_ref=dst, send_sem=send, recv_sem=recv, device_id=(device,), device_id_type=MESH)


def wait_bytes(ref, sem):
    pltpu.make_async_copy(ref, ref, sem).wait()


def step_kernel(
    nz, ny, nx, total_rows, protos_count, grad_coef, loss_coef,
    z_one, z_two, q_one, q_two, protos,
    codes_one, codes_two, loss_out, dz_one, dz_two, total,
    rows, cols, mat, wacc, rscale, csum, rs_buf, ex_buf, ag_buf,
    grads, g_buf, z_buf, part_buf, y_buf, yz_buf, sums, loss_buf,
    row_sem, col_sem, rs_send, rs_recv, ex_send, ex_recv, ag_send, ag_recv,
    z_send, z_recv, g_send, g_recv, p_send, p_recv, s_send, s_recv,
    az_send, az_recv, ay_send, ay_recv, ax_send, ax_recv, af_send, af_recv, pair_send, pair_recv,
    l_send, l_recv,
):
    me = lax.axis_index("data")
    core = lax.rem(me, CORES)
    chip = lax.div(me, CORES)
    plane = nx * ny
    yx = lax.rem(chip, plane)
    z = lax.div(chip, plane)
    x = lax.rem(yx, nx)
    y = lax.div(yx, nx)

    def dev(xx, yy, z2, cc):
        return ((z2 * ny + yy) * nx + xx) * CORES + cc

    members = nz * CORES
    mine = z * CORES + core
    tiles = mat.shape[1]
    per = tiles // members
    n_rows = mat.shape[2]
    batch = z_one.shape[0]
    wide = per * LANES
    blocks = 3 if n_rows % 24 == 0 else 1
    rb = n_rows // blocks
    unroll = 2

    def near(t):
        zz = lax.rem(z + near_offset(lax.div(t, 2)) + nz, nz)
        return zz * CORES + lax.rem(core + lax.rem(t, 2), CORES)

    member_offsets = [(dz, e) for dz in far_first(nz) for e in range(CORES)] + [(0, 1)]

    def member_at(dz, e):
        zz, cc = lax.rem(z + dz, nz), lax.rem(core + e, CORES)
        return zz * CORES + cc, dev(x, y, zz, cc)

    plane_offsets = [(dy, dx) for dy in range(ny) for dx in range(nx)][1:]
    plane_offsets.sort(key=lambda o: -(min(o[0], ny - o[0]) + min(o[1], nx - o[1])))

    def plane_at(dy, dx):
        yy, xx = lax.rem(y + dy, ny), lax.rem(x + dx, nx)
        return dev(xx, yy, z, core)

    views = ((z_one, q_one), (z_two, q_two))
    row_copies = [
        [pltpu.make_async_copy(zr, rows.at[v, pl.ds(0, batch)], row_sem.at[v, 0]),
         pltpu.make_async_copy(qr, rows.at[v, pl.ds(batch, n_rows - batch)], row_sem.at[v, 1])]
        for v, (zr, qr) in enumerate(views)]

    def slice_cols(m):
        return pl.ds(pl.multiple_of(m * wide, wide), wide)

    def col_copy(m):
        return pltpu.make_async_copy(protos.at[slice_cols(m)], cols.at[slice_cols(m)], col_sem.at[m])

    for c in row_copies[0]:
        c.start()
    for dz, e in member_offsets:
        col_copy(member_at(dz, e)[0]).start()
    col_copy(mine).start()
    for c in row_copies[1]:
        c.start()

    barrier = pltpu.get_barrier_semaphore()
    reached = [member_at(dz, e)[1] for dz, e in member_offsets] + [plane_at(*o) for o in plane_offsets]
    reached += [dev(lax.rem(x + d, nx), y, z, 1 - core) for d in range(1, nx)]
    reached += [dev(x, lax.rem(y + d, ny), z, 1 - core) for d in range(1, ny)]
    for device in reached:
        pl.semaphore_signal(barrier, inc=1, device_id=(device,), device_id_type=MESH)

    def rs_start(it, v, m, device):
        remote(csum.at[it, v, m], rs_buf.at[it, v, mine], rs_send.at[it, v], rs_recv.at[it, v], device).start()

    def rs_start_all(it, v):
        for dz, e in member_offsets:
            rs_start(it, v, *member_at(dz, e))

    def first_pass(v):
        for c in row_copies[v]:
            c.wait()

        def step(t, carry):
            ms = [near(members - 1 - (t * unroll + u)) for u in range(unroll)]
            if v == 0:
                for m in ms:
                    col_copy(m).wait()
            for m in ms:
                scores = dot_nt(rows[v], cols[slice_cols(m), :])
                for j in range(per):
                    e = jnp.exp2(scores[:, j * LANES:(j + 1) * LANES] * (LOG2E / EPSILON))
                    mat[v, m * per + j] = e
                    csum[0, v, m, pl.ds(j, 1), :] = jnp.sum(e, axis=0, keepdims=True)
            return carry

        lax.fori_loop(0, members // unroll, step, 0)

    first_pass(0)
    pl.semaphore_wait(barrier, len(reached))
    rs_start_all(0, 0)
    first_pass(1)
    rs_start_all(0, 1)

    def reduce_slice(it, v):
        wait_bytes(rs_buf.at[it, v, pl.ds(0, members - 1)], rs_recv.at[it, v])
        rs_buf[it, v, mine] = csum[it, v, mine]
        ex_buf[it, v, yx] = jnp.sum(rs_buf[it, v], axis=0)
        for o in plane_offsets:
            remote(ex_buf.at[it, v, yx], ex_buf.at[it, v, yx], ex_send.at[it, v], ex_recv.at[it, v], plane_at(*o)).start()

    def share_scale(it, v):
        wait_bytes(ex_buf.at[it, v, pl.ds(0, plane - 1)], ex_recv.at[it, v])
        ag_buf[it, v, mine] = 1.0 / (protos_count * jnp.sum(ex_buf[it, v], axis=0))
        for dz, e in member_offsets:
            remote(ag_buf.at[it, v, mine], ag_buf.at[it, v, mine], ag_send.at[it, v], ag_recv.at[it, v, mine],
                   member_at(dz, e)[1]).start()

    def wait_scale(it, v, m):
        wait_bytes(ag_buf.at[it, v, m], ag_recv.at[it, v, m])

    def next_pass(it, v):
        wacc[...] = jnp.zeros_like(wacc)

        def add_slice(t, carry):
            m = near(t)

            @pl.when(t > 0)
            def _():
                wait_scale(it, v, m)

            for b in range(blocks):
                part = pl.ds(b * rb, rb)
                acc = wacc[part, :]
                for j in range(per):
                    acc += mat[v, m * per + j, part, :] * ag_buf[it, v, m, pl.ds(j, 1), :]
                wacc[part, :] = acc
            return carry

        lax.fori_loop(0, members, add_slice, 0)
        row_sum = jnp.sum(wacc[...], axis=1, keepdims=True)
        rscale[...] = jnp.broadcast_to(1.0 / (total_rows * row_sum), rscale.shape)

        def col_slice(t, carry):
            m = near(members - 1 - t)
            acc = [None] * per
            for b in range(blocks):
                part = pl.ds(b * rb, rb)
                r = rscale[part, :]
                for j in range(per):
                    p = (mat[v, m * per + j, part, :] * r).reshape(rb // 8, 8, LANES).sum(axis=0)
                    acc[j] = p if acc[j] is None else acc[j] + p
            for j in range(per):
                csum[it + 1, v, m, pl.ds(j, 1), :] = jnp.sum(acc[j], axis=0, keepdims=True)

            @pl.when(t > 0)
            def _():
                before = near(members - t)
                rs_start(it + 1, v, before, dev(x, y, lax.div(before, CORES), lax.rem(before, CORES)))
            return carry

        lax.fori_loop(0, members, col_slice, 0)

    codes_refs = (codes_one, codes_two)
    width = g_buf.shape[4]
    chunks = grads.shape[0]

    def chunk_cols(t):
        return pl.ds(pl.multiple_of(t * width, width), width)

    def lane_fold(a):
        return sum(a[:, j:j + LANES] for j in range(0, a.shape[1], LANES))

    def softmax_terms(v):
        def step(t, acc):
            terms = jnp.exp2(dot_nt(rows[v, pl.ds(0, batch), :], cols[slice_cols(t), :]) * (LOG2E / TEMPERATURE))
            codes_refs[v][:, slice_cols(t)] = terms
            return acc + lane_fold(terms)
        acc = lax.fori_loop(0, members, step, jnp.zeros((batch, LANES), F32))
        return jnp.sum(acc, axis=1, keepdims=True)

    n_first, n_second = (nx, ny), (ny, nx)
    first, second = (x, y), (y, x)
    slot = [first[col] * CORES + core for col in range(2)]
    group = [n_first[col] * CORES for col in range(2)]

    def dev_first(col, f, cc):
        return dev(f, y, z, cc) if col == 0 else dev(x, f, z, cc)

    def dev_second(col, s):
        return dev(x, s, z, core) if col == 0 else dev(s, y, z, core)

    def first_offsets(col):
        return [(d, c) for d in far_first(n_first[col]) for c in range(CORES)] + [(0, 1)]

    def first_at(col, d, c):
        f, cc = lax.rem(first[col] + d, n_first[col]), lax.rem(core + c, CORES)
        return f * CORES + cc, dev_first(col, f, cc)

    def share_rows():
        for col in range(2):
            for v in range(2):
                z_buf[col, slot[col], pl.ds(v * batch, batch), :] = rows[v, pl.ds(0, batch), :]
            for o in first_offsets(col):
                for v in range(2):
                    remote(rows.at[v, pl.ds(0, batch)], z_buf.at[col, slot[col], pl.ds(v * batch, batch)],
                           z_send.at[col], z_recv.at[col], first_at(col, *o)[1]).start()

    share_rows()
    reduce_slice(0, 0)
    prob_sum = [softmax_terms(0)]
    reduce_slice(0, 1)
    share_scale(0, 0)
    prob_sum.append(softmax_terms(1))
    share_scale(0, 1)

    def iteration(it, carry):
        for v in range(2):
            next_pass(it, v)
        for v in range(2):
            reduce_slice(it + 1, v)
        for v in range(2):
            share_scale(it + 1, v)
        return carry

    lax.fori_loop(0, ITERS - 1, iteration, 0)
    last = ITERS - 1

    top = pl.ds(0, batch)

    def scaled(v, j):
        return mat[v, j, top, :] * ag_buf[last, v, lax.div(j, per), pl.ds(lax.rem(j, per), 1), :]

    def plan_sum(v):
        def step(t, acc):
            m = near(t)

            @pl.when(t > 0)
            def _():
                wait_scale(last, v, m)
            return acc + sum(mat[v, m * per + j, top, :] * ag_buf[last, v, m, pl.ds(j, 1), :] for j in range(per))
        acc = lax.fori_loop(0, members, step, jnp.zeros((batch, LANES), F32))
        return jnp.sum(acc, axis=1, keepdims=True)

    plan_inv = [1.0 / plan_sum(v) for v in range(2)]
    code_coef = [jnp.broadcast_to(plan_inv[v] * grad_coef, (batch, LANES)) for v in range(2)]
    prob_coef = [jnp.broadcast_to(grad_coef / prob_sum[v], (batch, LANES)) for v in range(2)]
    spread = width // LANES

    def g_start(col, h, m, device):
        block = (col * group[col] + m) * HALVES + h
        remote(grads.at[block], g_buf.at[col, h, slot[col]], g_send.at[col, h], g_recv.at[col, h], device).start()

    order = [(h, col) for h in range(HALVES) for col in range(2)]
    for h, col in order:
        def exchange_member(k):
            f = lax.rem(first[col] + near_offset(lax.div(k, 2)) + n_first[col], n_first[col])
            return f, lax.rem(core + lax.rem(k, 2), CORES)

        def make_block(t, carry, h=h, col=col, exchange_member=exchange_member):
            f, cc = exchange_member(group[col] - 1 - t)
            m = f * CORES + cc
            block = (col * group[col] + m) * HALVES + h
            for i in range(spread):
                j = block * spread + i
                lanes = pl.ds(pl.multiple_of(j * LANES, LANES), LANES)
                plans = [scaled(v, j) * code_coef[v] for v in range(2)]
                for v in range(2):
                    g = codes_refs[v][:, lanes] * prob_coef[v] - plans[1 - v]
                    grads[block, pl.ds(v * batch, batch), pl.ds(i * LANES, LANES)] = g.astype(BF16)

            @pl.when(t > 0)
            def _():
                f, cc = exchange_member(group[col] - t)
                g_start(col, h, f * CORES + cc, dev_first(col, f, cc))
            return carry

        lax.fori_loop(0, group[col], make_block, 0)
        g_buf[col, h, slot[col]] = grads[(col * group[col] + slot[col]) * HALVES + h]

    lse = [jnp.log(prob_sum[v]) for v in range(2)]

    def finish(t, carry):
        loss, dz = carry
        scores = [dot_nt(rows[v, top, :], cols[chunk_cols(t), :]) for v in range(2)]
        for i in range(spread):
            j = t * spread + i
            lanes = pl.ds(pl.multiple_of(j * LANES, LANES), LANES)
            for v in range(2):
                codes = scaled(v, j) * plan_inv[v]
                codes_refs[v][:, lanes] = codes
                other = scores[1 - v][:, i * LANES:(i + 1) * LANES]
                loss = loss + codes * (other * (1.0 / TEMPERATURE) - lse[1 - v])
        dz = dz + jnp.dot(grads[t], cols[chunk_cols(t), :], preferred_element_type=F32)
        return loss, dz

    loss, dz = lax.fori_loop(0, chunks, finish, (jnp.zeros((batch, LANES), F32), jnp.zeros((2 * batch, cols.shape[1]), F32)))
    dz_one[...] = dz[:batch]
    dz_two[...] = dz[batch:]
    loss_buf[0, slot[0]] = jnp.sum(loss, axis=0, keepdims=True)
    for o in first_offsets(0):
        remote(loss_buf.at[0, slot[0]], loss_buf.at[0, slot[0]], l_send.at[0], l_recv.at[0], first_at(0, *o)[1]).start()

    block_rows = [width // n_second[col] for col in range(2)]
    unit = block_rows[0] // nz

    def address(col, h, f, cc, s, zi):
        half_count = total.shape[0] // 2
        return col * half_count + ((f * CORES + cc) * HALVES + h) * width + s * block_rows[col] + zi * unit

    def rows_of(addr, n):
        return pl.ds(pl.multiple_of(addr, 8), n)

    def stage_g(h, col):
        wait_bytes(g_buf.at[col, h, pl.ds(0, group[col] - 1)], g_recv.at[col, h])
        if h == 0:
            wait_bytes(z_buf.at[col, pl.ds(0, group[col] - 1)], z_recv.at[col])
        k = group[col] * z_buf.shape[2]
        g = g_buf[col, h].reshape(k, width)
        zs = z_buf[col].reshape(k, z_buf.shape[3])
        part_buf[col, h] = lax.dot_general(g, zs, (((0,), (0,)), ((), ())), preferred_element_type=F32)
        for d in far_first(n_second[col]):
            s = lax.rem(second[col] + d, n_second[col])
            remote(part_buf.at[col, h, rows_of(s * block_rows[col], block_rows[col])], y_buf.at[col, h, second[col]],
                   p_send.at[col, h], p_recv.at[col, h], dev_second(col, s)).start()

    def stage_y(h, col):
        wait_bytes(y_buf.at[col, h, pl.ds(0, n_second[col] - 1)], p_recv.at[col, h])
        y_buf[col, h, second[col]] = part_buf[col, h, rows_of(second[col] * block_rows[col], block_rows[col])]
        yz_buf[col, h, 0] = jnp.sum(y_buf[col, h], axis=0)
        for d in far_first(nz):
            z2 = lax.rem(z + d, nz)
            remote(yz_buf.at[col, h, 0, rows_of(z2 * unit, unit)], sums.at[col, h, z],
                   s_send.at[col, h], s_recv.at[col, h], dev(x, y, z2, core)).start()

    def stage_z(h, col):
        wait_bytes(sums.at[col, h, pl.ds(0, nz - 1)], s_recv.at[col, h])
        sums[col, h, z] = yz_buf[col, h, 0, rows_of(z * unit, unit)]
        own = rows_of(address(col, h, first[col], core, second[col], z), unit)
        total[own, :] = jnp.sum(sums[col, h], axis=0)
        for d in far_first(nz):
            z2 = lax.rem(z + d, nz)
            remote(total.at[own], total.at[own], az_send.at[col, h], az_recv.at[col, h], dev(x, y, z2, core)).start()

    def stage_az(h, col):
        block = rows_of(address(col, h, first[col], core, second[col], 0), block_rows[col])
        wait_bytes(total.at[pl.ds(0, (nz - 1) * unit)], az_recv.at[col, h])
        for d in far_first(n_second[col]):
            s = lax.rem(second[col] + d, n_second[col])
            remote(total.at[block], total.at[block], ay_send.at[col, h], ay_recv.at[col, h], dev_second(col, s)).start()

    def pair_start(h, col, k, part):
        remote(total.at[part], total.at[part], pair_send.at[col, h, k], pair_recv.at[col, h, k],
               dev(x, y, z, 1 - core)).start()

    def stage_ay(h, col):
        n1 = n_first[col]
        wait_bytes(total.at[pl.ds(0, (n_second[col] - 1) * block_rows[col])], ay_recv.at[col, h])
        whole = rows_of(address(col, h, first[col], core, 0, 0), width)
        for d, step in enumerate((1, n1 - 1)):
            f = lax.rem(first[col] + step, n1)
            remote(total.at[whole], total.at[whole], ax_send.at[col, h, d], ax_recv.at[col, h, d],
                   dev_first(col, f, core)).start()
        pair_start(h, col, 0, whole)

    def stage_ax(h, col):
        n1 = n_first[col]
        for d, step in enumerate((1, n1 - 1)):
            src = lax.rem(first[col] + n1 - step, n1)
            nxt = lax.rem(first[col] + step, n1)
            whole = rows_of(address(col, h, src, core, 0, 0), width)
            wait_bytes(total.at[whole], ax_recv.at[col, h, d])
            part = rows_of(address(col, h, src, core, 0, 0) + d * (width // 2), width // 2)
            remote(total.at[part], total.at[part], af_send.at[col, h, d], af_recv.at[col, h, d],
                   dev_first(col, nxt, core)).start()
            pair_start(h, col, 1 + d, whole)

    def stage_af(h, col):
        n1 = n_first[col]
        src = lax.rem(first[col] + n1 // 2, n1)
        for d in range(2):
            part = rows_of(address(col, h, src, core, 0, 0) + d * (width // 2), width // 2)
            wait_bytes(total.at[part], af_recv.at[col, h, d])
            pair_start(h, col, 3 + d, part)

    def loss_stage(k):
        if k == 0:
            wait_bytes(loss_buf.at[0, pl.ds(0, group[0] - 1)], l_recv.at[0])
            loss_buf[1, y] = jnp.sum(loss_buf[0, pl.ds(0, group[0])], axis=0)
            for d in range(1, ny):
                remote(loss_buf.at[1, y], loss_buf.at[1, y], l_send.at[1], l_recv.at[1],
                       dev(x, lax.rem(y + d, ny), z, core)).start()
        elif k == 1:
            wait_bytes(loss_buf.at[1, pl.ds(0, ny - 1)], l_recv.at[1])
            loss_buf[2, z] = jnp.sum(loss_buf[1, pl.ds(0, ny)], axis=0)
            for d in range(1, nz):
                remote(loss_buf.at[2, z], loss_buf.at[2, z], l_send.at[2], l_recv.at[2],
                       dev(x, y, lax.rem(z + d, nz), core)).start()
        else:
            wait_bytes(loss_buf.at[2, pl.ds(0, nz - 1)], l_recv.at[2])
            terms = jnp.sum(loss_buf[2, pl.ds(0, nz)], axis=0)
            loss_out[...] = jnp.sum(terms, axis=1, keepdims=True) * loss_coef

    stages = [(stage_g, 0), (stage_y, 5), (stage_z, 10), (stage_az, 15), (stage_ay, 20), (stage_ax, 26), (stage_af, 30)]
    steps = sorted((at + 6 * h, k, h, col) for k, (_, at) in enumerate(stages) for h, col in order)
    for _, k, h, col in steps:
        stages[k][0](h, col)
        if (h, col) == (1, 1) and k < 3:
            loss_stage(k)

    for h, col in order:
        n1 = n_first[col]
        for k, src, off, n in (
            (0, first[col], 0, width),
            (1, lax.rem(first[col] + n1 - 1, n1), 0, width),
            (2, lax.rem(first[col] + 1, n1), 0, width),
            (3, lax.rem(first[col] + n1 // 2, n1), 0, width // 2),
            (4, lax.rem(first[col] + n1 // 2, n1), width // 2, width // 2),
        ):
            part = rows_of(address(col, h, src, 1 - core, 0, 0) + off, n)
            wait_bytes(total.at[part], pair_recv.at[col, h, k])
            wait_bytes(total.at[part], pair_send.at[col, h, k])

    def drain(it, carry):
        for v in range(2):
            wait_bytes(rs_buf.at[it, v, pl.ds(0, members - 1)], rs_send.at[it, v])
            wait_bytes(ex_buf.at[it, v, pl.ds(0, plane - 1)], ex_send.at[it, v])
            wait_bytes(rs_buf.at[it, v, pl.ds(0, members - 1)], ag_send.at[it, v])
        return carry

    lax.fori_loop(0, ITERS, drain, 0)
    for col in range(2):
        wait_bytes(z_buf.at[col, pl.ds(0, group[col] - 1)], z_send.at[col])
        for h in range(HALVES):
            wait_bytes(g_buf.at[col, h, pl.ds(0, group[col] - 1)], g_send.at[col, h])
            wait_bytes(y_buf.at[col, h, pl.ds(0, n_second[col] - 1)], p_send.at[col, h])
            wait_bytes(sums.at[col, h, pl.ds(0, nz - 1)], s_send.at[col, h])
            wait_bytes(total.at[pl.ds(0, (nz - 1) * unit)], az_send.at[col, h])
            wait_bytes(total.at[pl.ds(0, (n_second[col] - 1) * block_rows[col])], ay_send.at[col, h])
            for d in range(2):
                wait_bytes(total.at[pl.ds(0, width)], ax_send.at[col, h, d])
                wait_bytes(total.at[pl.ds(0, width // 2)], af_send.at[col, h, d])
    wait_bytes(loss_buf.at[0, pl.ds(0, group[0] - 1)], l_send.at[0])
    wait_bytes(loss_buf.at[1, pl.ds(0, ny - 1)], l_send.at[1])
    wait_bytes(loss_buf.at[2, pl.ds(0, nz - 1)], l_send.at[2])


def fused_step(nz, ny, nx, z_one, z_two, q_one, q_two, protos):
    batch, dim = z_one.shape
    n_rows = batch + q_one.shape[0]
    count = protos.shape[0]
    tiles = count // LANES
    members = nz * CORES
    plane = nx * ny
    devices = plane * members
    small = (tiles // members, LANES)
    group = nx * CORES
    chunks = 2 * HALVES * group
    width = count // chunks
    any_spec = pl.BlockSpec(memory_space=pl.ANY)
    vmem = pl.BlockSpec(memory_space=pltpu.VMEM)
    dma = pltpu.SemaphoreType.DMA
    two = dma((2, HALVES))
    out_bytes = 4 * (2 * batch * count + 2 * batch * dim + count * dim)
    return pl.pallas_call(
        functools.partial(
            step_kernel, nz, ny, nx, float(devices * n_rows), float(count),
            1.0 / (2 * devices * batch * TEMPERATURE), -1.0 / (2 * devices * batch)),
        out_shape=(
            pltpu.VMEM((batch, count), F32),
            pltpu.VMEM((batch, count), F32),
            pltpu.VMEM((1, 1), F32),
            pltpu.VMEM((batch, dim), F32),
            pltpu.VMEM((batch, dim), F32),
            pltpu.VMEM((count, dim), F32),
        ),
        in_specs=[any_spec] * 5,
        out_specs=(vmem,) * 6,
        scratch_shapes=[
            pltpu.VMEM((2, n_rows, dim), BF16),
            pltpu.VMEM((count, dim), BF16),
            pltpu.VMEM((2, tiles, n_rows, LANES), F32),
            pltpu.VMEM((n_rows, LANES), F32),
            pltpu.VMEM((n_rows, LANES), F32),
            pltpu.VMEM((ITERS, 2, members) + small, F32),
            pltpu.VMEM((ITERS, 2, members) + small, F32),
            pltpu.VMEM((ITERS, 2, plane) + small, F32),
            pltpu.VMEM((ITERS, 2, members) + small, F32),
            pltpu.VMEM((chunks, 2 * batch, width), BF16),
            pltpu.VMEM((2, HALVES, group, 2 * batch, width), BF16),
            pltpu.VMEM((2, group, 2 * batch, dim), BF16),
            pltpu.VMEM((2, HALVES, width, dim), F32),
            pltpu.VMEM((2, HALVES, ny, width // ny, dim), F32),
            pltpu.VMEM((2, HALVES, 1, width // ny, dim), F32),
            pltpu.VMEM((2, HALVES, nz, width // ny // nz, dim), F32),
            pltpu.VMEM((3, max(group, nz), 1, LANES), F32),
            dma((2, 2)),
            dma((members,)),
            dma((ITERS, 2)), dma((ITERS, 2)), dma((ITERS, 2)), dma((ITERS, 2)), dma((ITERS, 2)),
            dma((ITERS, 2, members)),
            dma((2,)), dma((2,)),
            two, two, two, two, two, two, two, two, two, two,
            dma((2, HALVES, 2)), dma((2, HALVES, 2)), dma((2, HALVES, 2)), dma((2, HALVES, 2)),
            dma((2, HALVES, 5)), dma((2, HALVES, 5)),
            dma((3,)), dma((3,)),
        ],
        compiler_params=pltpu.CompilerParams(
            collective_id=0, has_side_effects=True, vmem_limit_bytes=VMEM_TOTAL - out_bytes - 2 ** 16),
        name="step",
    )(z_one, z_two, q_one, q_two, protos)


def flush(arrays):
    n = len(arrays)

    def kernel(*refs):
        sem = refs[-1]
        copies = [pltpu.make_async_copy(refs[i], refs[n + i], sem.at[i]) for i in range(n)]
        for c in copies:
            c.start()
        for c in copies:
            c.wait()

    return pl.pallas_call(
        kernel,
        out_shape=tuple(jax.ShapeDtypeStruct(a.shape, a.dtype) for a in arrays),
        in_specs=[pl.BlockSpec(memory_space=pltpu.VMEM)] * n,
        out_specs=(pl.BlockSpec(memory_space=pltpu.HBM),) * n,
        scratch_shapes=[pltpu.SemaphoreType.DMA((n,))],
        compiler_params=pltpu.CompilerParams(vmem_limit_bytes=2 ** 20),
        name="flush",
    )(*(pltpu.with_memory_space_constraint(a, pltpu.VMEM) for a in arrays))


def solution(mesh, nz=CHIPS_Z, nx=CHIPS_X):
    ny = mesh.shape["data"] // (nz * nx * CORES)

    def local_step(z_one, z_two, protos, queue_one, queue_two):
        outs = fused_step(nz, ny, nx, z_one, z_two, queue_one, queue_two, protos)
        codes_one, codes_two, loss, dz_one, dz_two, grad_protos = flush(outs)
        return codes_one, codes_two, loss.reshape(()), dz_one, dz_two, grad_protos

    row_spec = P("data", None)
    full_spec = P(None, None)
    return jax.shard_map(
        local_step,
        mesh=mesh,
        in_specs=(row_spec, row_spec, full_spec, row_spec, row_spec),
        out_specs=(row_spec, row_spec, P(), row_spec, row_spec, full_spec),
        check_vma=False,
    )
```

time: 389 us -> 133 us (0.34)
  waiting for transfers between devices: 190 us -> 0 us
  blocking collectives: 74.7 us -> 0 us
  Pallas kernels: 66.9 us -> 132 us
  matrix products: 20.5 us -> 0 us
  between operations: 17.3 us -> 0.64 us
  other arithmetic: 10.7 us -> 0 us
  local copies, waits for them, and re-layouts: 8.32 us -> 0 us
    psum x1 -> x0, waiting for transfers between devices: 190 us -> none  [local_step(): grad_protos = lax.psum(proto_part, 'data')]
    psum x1 -> x0, blocking collectives: 74.7 us -> none  [local_step(): swap_loss = -lax.psum(part_loss, 'data') / (2 * batch_total)]
    pallas_call x1 -> x2, Pallas kernels: 66.9 us -> 132 us  [the longest x1 126 us: fused_step(): pl.pallas_call(functools.partial(step_kernel, nz, ny, nx, float(devices *...]
    dot_general x6 -> x0, matrix products: 20.5 us -> none  [the longest x2 9.03 us: dot_nt(): lax.dot_general(a, b, (((1,), (1,)), ((), ())), preferred_element_type=F32)]
    reduce_sum x4 -> x0, other arithmetic: 7.61 us -> none  [the longest x2 4.56 us: local_step(): part_loss = jnp.sum(codes_two * logp_one) + jnp.sum(codes_one * logp_two)]
    unnamed x23 -> x0, local copies, waits for them, and re-layouts: 7.38 us -> none
  transfers between devices with their start and end apart: 1 -> 0, of which waited for: 1 -> 0; matrix products, arithmetic and copies ran while one was open for 2% -> 0% of each run, Pallas kernels for 0% -> 0%
where the time goes in v3:
time: 133 us; the launch traced here: 132 us
  Pallas kernels  132 us (99%)
    pallas_call x1, Pallas kernels, fused_step(): pl.pallas_call(functools.partial(step_kernel, nz, ny, nx, float(devices *...  126 us
    pallas_call x1, Pallas kernels, flush(): pl.pallas_call(kernel, out_shape=tuple((jax.ShapeDtypeStruct(a.shape, a.d...  5.5 us

profile of v3, /device:TPU:1, one launch (start us, length us, event | category | flops | bytes accessed | tf_op | source)
XLA Modules:
  0.0 132.5 jit_solution(2842321301314373583)
XLA Ops:
  0.6 126.3 %step.1 = (f32[64,8192]{1,0:T(8,128)S(1)}, f32[64,8192]{1,0:T(8,128)S(1)}, f32[1,1]{1,0:T(1,128)}, f32[64,256]{1,0:T(8,128)S(1)}, f32[64,256]{1,0:T(8,128)S(1)}, /*index=5*/f32[8192,256]{1,0:T(8,128)S(1)}) custom-call(bf16[64,256]{1,0:T(8,128)(2,1)} %z_one.1, bf16[64,256]{1,0:T(8,128)(2,1)} %z_two.1, bf16[512,256]{1,0:T(8,128)(2,1)} %q_one.1, ...), custom_call_target="tpu_custom_call" | custom-call | tf_op jit(solution)/shard_map/step/pallas_call | solution.py:516
  127.0 5.5 %flush.1 = (f32[64,8192]{1,0:T(8,128)}, f32[64,8192]{1,0:T(8,128)}, f32[1,1]{1,0:T(1,128)}, f32[64,256]{1,0:T(8,128)}, f32[64,256]{1,0:T(8,128)}, /*index=5*/f32[8192,256]{1,0:T(8,128)}) custom-call(f32[64,8192]{1,0:T(8,128)S(1)} %get-tuple-element.18.refs_0_, f32[64,8192]{1,0:T(8,128)S(1)} %get-tuple-element.19.refs_1_, f32[1,1]{1,0:T(1,128)} %get-tuple-element.20.refs_2_, ...), custom_call_target="tpu_custom_call" | custom-call | tf_op jit(solution)/shard_map/flush/pallas_call | solution.py:575

commit v4 on v3

--- a/solution.py
+++ b/solution.py
@@ -75,7 +75,7 @@
     wide = per * LANES
     blocks = 3 if n_rows % 24 == 0 else 1
     rb = n_rows // blocks
-    unroll = 2
+    unroll = 4 if members % 4 == 0 else 1
 
     def near(t):
         zz = lax.rem(z + near_offset(lax.div(t, 2)) + nz, nz)
@@ -171,29 +171,26 @@
         wait_bytes(ag_buf.at[it, v, m], ag_recv.at[it, v, m])
 
     def next_pass(it, v):
-        wacc[...] = jnp.zeros_like(wacc)
-
-        def add_slice(t, carry):
-            m = near(t)
-
-            @pl.when(t > 0)
-            def _():
-                wait_scale(it, v, m)
-
+        def add_slice(m, fresh):
             for b in range(blocks):
                 part = pl.ds(b * rb, rb)
-                acc = wacc[part, :]
+                acc = None if fresh else wacc[part, :]
                 for j in range(per):
-                    acc += mat[v, m * per + j, part, :] * ag_buf[it, v, m, pl.ds(j, 1), :]
+                    term = mat[v, m * per + j, part, :] * ag_buf[it, v, m, pl.ds(j, 1), :]
+                    acc = term if acc is None else acc + term
                 wacc[part, :] = acc
-            return carry
-
-        lax.fori_loop(0, members, add_slice, 0)
+
+        def add_next(t, m):
+            wait_scale(it, v, m)
+            add_slice(m, False)
+            return near(t + 1)
+
+        add_slice(mine, True)
+        lax.fori_loop(1, members, add_next, near(1))
         row_sum = jnp.sum(wacc[...], axis=1, keepdims=True)
         rscale[...] = jnp.broadcast_to(1.0 / (total_rows * row_sum), rscale.shape)
 
-        def col_slice(t, carry):
-            m = near(members - 1 - t)
+        def col_slice(m):
             acc = [None] * per
             for b in range(blocks):
                 part = pl.ds(b * rb, rb)
@@ -204,13 +201,14 @@
             for j in range(per):
                 csum[it + 1, v, m, pl.ds(j, 1), :] = jnp.sum(acc[j], axis=0, keepdims=True)
 
-            @pl.when(t > 0)
-            def _():
-                before = near(members - t)
-                rs_start(it + 1, v, before, dev(x, y, lax.div(before, CORES), lax.rem(before, CORES)))
-            return carry
-
-        lax.fori_loop(0, members, col_slice, 0)
+        def col_next(t, carry):
+            before, m = carry
+            col_slice(m)
+            rs_start(it + 1, v, before, dev(x, y, lax.div(before, CORES), lax.rem(before, CORES)))
+            return m, near(members - 2 - t)
+
+        col_slice(near(members - 1))
+        lax.fori_loop(1, members, col_next, (near(members - 1), near(members - 2)))
 
     codes_refs = (codes_one, codes_two)
     width = g_buf.shape[4]
@@ -224,10 +222,13 @@
 
     def softmax_terms(v):
         def step(t, acc):
-            terms = jnp.exp2(dot_nt(rows[v, pl.ds(0, batch), :], cols[slice_cols(t), :]) * (LOG2E / TEMPERATURE))
-            codes_refs[v][:, slice_cols(t)] = terms
-            return acc + lane_fold(terms)
-        acc = lax.fori_loop(0, members, step, jnp.zeros((batch, LANES), F32))
+            for u in range(2):
+                part = slice_cols(t * 2 + u)
+                terms = jnp.exp2(dot_nt(rows[v, pl.ds(0, batch), :], cols[part, :]) * (LOG2E / TEMPERATURE))
+                codes_refs[v][:, part] = terms
+                acc = acc + lane_fold(terms)
+            return acc
+        acc = lax.fori_loop(0, members // 2, step, jnp.zeros((batch, LANES), F32))
         return jnp.sum(acc, axis=1, keepdims=True)
 
     n_first, n_second = (nx, ny), (ny, nx)
@@ -331,7 +332,7 @@
 
     lse = [jnp.log(prob_sum[v]) for v in range(2)]
 
-    def finish(t, carry):
+    def finish_chunk(t, carry):
         loss, dz = carry
         scores = [dot_nt(rows[v, top, :], cols[chunk_cols(t), :]) for v in range(2)]
         for i in range(spread):
@@ -345,7 +346,10 @@
         dz = dz + jnp.dot(grads[t], cols[chunk_cols(t), :], preferred_element_type=F32)
         return loss, dz
 
-    loss, dz = lax.fori_loop(0, chunks, finish, (jnp.zeros((batch, LANES), F32), jnp.zeros((2 * batch, cols.shape[1]), F32)))
+    def finish(t, carry):
+        return finish_chunk(t * 2 + 1, finish_chunk(t * 2, carry))
+
+    loss, dz = lax.fori_loop(0, chunks // 2, finish, (jnp.zeros((batch, LANES), F32), jnp.zeros((2 * batch, cols.shape[1]), F32)))
     dz_one[...] = dz[:batch]
     dz_two[...] = dz[batch:]
     loss_buf[0, slot[0]] = jnp.sum(loss, axis=0, keepdims=True)
@@ -561,12 +565,18 @@
     )(z_one, z_two, q_one, q_two, protos)
 
 
-def flush(arrays):
+def flush(arrays, piece=2 ** 20):
     n = len(arrays)
+    cuts = []
+    for i, a in enumerate(arrays):
+        parts = max(1, 4 * a.size // piece)
+        cuts += [(i, k * (a.shape[0] // parts), a.shape[0] // parts) for k in range(parts)]
 
     def kernel(*refs):
         sem = refs[-1]
-        copies = [pltpu.make_async_copy(refs[i], refs[n + i], sem.at[i]) for i in range(n)]
+        copies = [
+            pltpu.make_async_copy(refs[i].at[pl.ds(at, count)], refs[n + i].at[pl.ds(at, count)], sem.at[k])
+            for k, (i, at, count) in enumerate(cuts)]
         for c in copies:
             c.start()
         for c in copies:
@@ -577,7 +587,7 @@
         out_shape=tuple(jax.ShapeDtypeStruct(a.shape, a.dtype) for a in arrays),
         in_specs=[pl.BlockSpec(memory_space=pltpu.VMEM)] * n,
         out_specs=(pl.BlockSpec(memory_space=pltpu.HBM),) * n,
-        scratch_shapes=[pltpu.SemaphoreType.DMA((n,))],
+        scratch_shapes=[pltpu.SemaphoreType.DMA((len(cuts),))],
         compiler_params=pltpu.CompilerParams(vmem_limit_bytes=2 ** 20),
         name="flush",
     )(*(pltpu.with_memory_space_constraint(a, pltpu.VMEM) for a in arrays))

time: 133 us -> 129 us (0.970)
  Pallas kernels: 132 us -> 129 us
    pallas_call x1, Pallas kernels: 126 us -> 123 us  [fused_step(): pl.pallas_call(functools.partial(step_kernel, nz, ny, nx, float(devices *...]
where the time goes in v4:
time: 129 us
  Pallas kernels  129 us (100%)
    pallas_call x1, Pallas kernels, fused_step(): pl.pallas_call(functools.partial(step_kernel, nz, ny, nx, float(devices *...  123 us
    pallas_call x1, Pallas kernels, flush(): pl.pallas_call(kernel, out_shape=tuple((jax.ShapeDtypeStruct(a.shape, a.d...  5.37 us

profile of v4, /device:TPU:1, one launch (start us, length us, event | category | flops | bytes accessed | tf_op | source)
XLA Modules:
  0.0 129.3 jit_solution(6943022415872251160)
XLA Ops:
  0.6 123.3 %step.1 = (f32[64,8192]{1,0:T(8,128)S(1)}, f32[64,8192]{1,0:T(8,128)S(1)}, f32[1,1]{1,0:T(1,128)}, f32[64,256]{1,0:T(8,128)S(1)}, f32[64,256]{1,0:T(8,128)S(1)}, /*index=5*/f32[8192,256]{1,0:T(8,128)S(1)}) custom-call(bf16[64,256]{1,0:T(8,128)(2,1)} %z_one.1, bf16[64,256]{1,0:T(8,128)(2,1)} %z_two.1, bf16[512,256]{1,0:T(8,128)(2,1)} %q_one.1, ...), custom_call_target="tpu_custom_call" | custom-call | tf_op jit(solution)/shard_map/step/pallas_call | solution.py:520
  124.0 5.4 %flush.1 = (f32[64,8192]{1,0:T(8,128)}, f32[64,8192]{1,0:T(8,128)}, f32[1,1]{1,0:T(1,128)}, f32[64,256]{1,0:T(8,128)}, f32[64,256]{1,0:T(8,128)}, /*index=5*/f32[8192,256]{1,0:T(8,128)}) custom-call(f32[64,8192]{1,0:T(8,128)S(1)} %get-tuple-element.18.refs_0_, f32[64,8192]{1,0:T(8,128)S(1)} %get-tuple-element.19.refs_1_, f32[1,1]{1,0:T(1,128)} %get-tuple-element.20.refs_2_, ...), custom_call_target="tpu_custom_call" | custom-call | tf_op jit(solution)/shard_map/flush/pallas_call | solution.py:585
